TPU v7x, 32 devices: a whole 2x2x4 slice. The times are simulated.
32 devices in a mesh: tp: 8 (over z, y), fsdp: 4 (over x, core).
Axes of the slice: x: 2, y: 2, z: 4, core: 2. Of those that a mesh axis runs over, the one named last changes fastest.
Arguments:
- hidden: bfloat16 [8192, 1024], P('fsdp')
- labels: int32 [8192], P('fsdp')
- tok_mask: float32 [8192], P('fsdp')
- norm_gain: bfloat16 [1024], replicated
- w_head: bfloat16 [1024, 151936], P('fsdp', 'tp')
Outputs:
- output 1: float32 [], replicated
- output 2: bfloat16 [8192, 1024], P('fsdp')
- output 3: bfloat16 [1024, 151936], P('fsdp', 'tp')
- output 4: float32 [1024], replicated
All inputs are finite; a program needn't handle non-finite values.
Results may differ from a plain program's by a relative error of at most 0.0132744.
Values are sent between devices in bfloat16 or wider.
A program may use at most 1 GiB of HBM per device.

v0:
```python
import jax
import jax.numpy as jnp
from jax import lax
from jax.sharding import PartitionSpec as P, NamedSharding

NORM_EPS = 1e-6


def solution(mesh):
    def per_device(hidden, labels, tok_mask, norm_gain, w_rows):
        w_cols = lax.all_gather(w_rows, 'fsdp', axis=0, tiled=True)
        vocab_local = w_cols.shape[1]
        hidden_f32 = hidden.astype(jnp.float32)
        gain_f32 = norm_gain.astype(jnp.float32)
        inv_rms = lax.rsqrt(jnp.mean(hidden_f32 * hidden_f32, axis=-1, keepdims=True) + NORM_EPS)
        normed = hidden_f32 * inv_rms
        z_rows = (normed * gain_f32).astype(jnp.bfloat16)
        logits = jnp.dot(z_rows, w_cols, preferred_element_type=jnp.float32)
        local_label = labels - lax.axis_index('tp') * vocab_local
        label_hit = jnp.arange(vocab_local)[None, :] == local_label[:, None]
        row_max = lax.pmax(jnp.max(logits, axis=1), 'tp')
        part_stats = jnp.stack([jnp.sum(jnp.exp(logits - row_max[:, None]), axis=1), jnp.sum(jnp.where(label_hit, logits, 0.0), axis=1)])
        tok_stats = lax.psum(part_stats, 'tp')
        log_norm = row_max + jnp.log(tok_stats[0])
        tok_loss = log_norm - tok_stats[1]
        loss_totals = lax.psum(jnp.stack([jnp.sum(tok_mask * tok_loss), jnp.sum(tok_mask)]), 'fsdp')
        mean_loss = loss_totals[0] / loss_totals[1]
        tok_scale = tok_mask / loss_totals[1]
        d_logits = ((jnp.exp(logits - log_norm[:, None]) - label_hit.astype(jnp.float32)) * tok_scale[:, None]).astype(jnp.bfloat16)
        grad_part = jnp.einsum('tv,dv->td', d_logits, w_cols, preferred_element_type=jnp.float32).astype(jnp.bfloat16)
        grad_z = lax.psum(grad_part, 'tp').astype(jnp.float32)
        grad_gain = lax.psum(jnp.sum(grad_z * normed, axis=0), 'fsdp')
        d_normed = grad_z * gain_f32
        grad_hid = inv_rms * (d_normed - normed * jnp.mean(d_normed * normed, axis=-1, keepdims=True))
        dw_part = jnp.einsum('td,tv->dv', z_rows, d_logits, preferred_element_type=jnp.float32)
        grad_head = lax.psum_scatter(dw_part, 'fsdp', scatter_dimension=0, tiled=True)
        return mean_loss, grad_hid.astype(jnp.bfloat16), grad_head.astype(jnp.bfloat16), grad_gain

    return jax.shard_map(per_device, mesh=mesh, in_specs=(P('fsdp', None), P('fsdp'), P('fsdp'), P(), P('fsdp', 'tp')), out_specs=(P(), P('fsdp', None), P('fsdp', 'tp'), P()), check_vma=False)
```

profile of v0, /device:TPU:0, one launch (start us, length us, event | category | flops | bytes accessed | tf_op | source)
XLA Modules:
  0.0 2053.2 jit_solution(6480197588172216871)
XLA Ops:
  7.2 0.0 copy-start.10
  7.2 0.0 copy-start.9
  7.2 0.0 copy-start.8
  7.2 0.0 all-gather.2.cloned.1.call-start
  7.2 0.7 all-gather.2.cloned.1.call-update
  7.9 0.0 all-reduce.5.cloned.1.call-start
  8.0 0.0 copy-done.9
  8.0 0.0 copy-start.4
  8.0 0.0 copy-done.10
  8.0 0.7 dynamic-slice
  8.7 3.1 fusion.8
  11.8 0.0 copy-done.8
  11.8 0.0 copy-start.2
  11.8 0.6 broadcast_subtract_fusion
  12.4 239.1 %all-gather.2.cloned.1.call-done = bf16[1024,18992]{0,1:T(8,128)(2,1)} async-done(((bf16[256,18992]{0,1:T(8,128)(2,1)}), bf16[1024,18992]{0,1:T(8,128)(2,1)}) %all-gather.2.cloned.1.call-update) | async-done | bytes 38895632 | tf_op jit(solution)/shard_map/all_gather | solution.py:11
  251.5 0.0 copy-start.6
  251.5 93.6 %fusion.15 = (f32[2048]{0:T(1024)S(1)}, f32[2048,18992]{0,1:T(8,128)}) fusion(bf16[1024,18992]{0,1:T(8,128)(2,1)} %all-gather.2.cloned.1.call-done, bf16[2048,1024]{1,0:T(8,128)(2,1)} %param.5, f32[1024]{0:T(1024)S(1)} %convert_element_type.28, f32[2048]{0:T(1024)S(1)} %add_rsqrt_fusion), kind=kOutput, calls=%fused_computation.31 | convolution fusion | flops 79705505792 | bytes 198692864 | tf_op jit(solution)/shard_map/dot_general | solution.py:18
  345.1 0.0 copy-done.4
  345.1 0.0 copy-done.2
  345.1 21.6 %pmax.7 = f32[2048]{0:T(1024)S(1)} all-reduce(f32[2048]{0:T(1024)S(1)} %get-tuple-element.17), channel_id=1, replica_groups=mesh['tp'=8,'fsdp'=4] {'tp'}, use_global_device_ids=true, to_apply=%region_2.0 | all-reduce | flops 2048 | bytes 16384 | tf_op jit(solution)/shard_map/pmax | solution.py:21
  366.7 0.0 copy-done.6
  366.7 0.0 copy-start.7
  366.7 47.7 %exponential_reduce_fusion = (f32[2048]{0:T(1024)S(1)}, f32[2048]{0:T(1024)S(1)}) fusion(f32[2048,18992]{0,1:T(8,128)} %get-tuple-element.18, f32[2048]{0:T(1024)S(1)} %pmax.7, s32[2048]{0:T(1024)S(1)} %copy-done.6), kind=kLoop, calls=%fused_computation.3 | loop fusion | flops 194473984 | bytes 155615232 | tf_op jit(solution)/shard_map/reduce_sum | solution.py:22
  414.5 33.0 %psum.28 = f32[2,2048]{1,0:T(2,128)S(1)} all-reduce(f32[2,2048]{1,0:T(2,128)S(1)} %pad_maximum_fusion), channel_id=1, replica_groups=mesh['tp'=8,'fsdp'=4] {'tp'}, use_global_device_ids=true, to_apply=%region_5.6 | all-reduce | flops 4096 | bytes 32768 | tf_op jit(solution)/shard_map/psum | solution.py:23
  447.5 0.0 copy-done.7
  447.5 0.6 multiply_reduce_fusion
  448.1 1.4 pad_maximum_fusion.1
  450.2 6.1 psum.29
  456.3 0.6 fusion.14
  456.9 0.6 broadcast_divide_fusion
  457.6 0.0 copy-start.3
  457.6 0.0 copy-start.5
  457.6 110.5 %convolution_convert_fusion = bf16[2048,1024]{1,0:T(8,128)(2,1)} fusion(bf16[1024,18992]{0,1:T(8,128)(2,1)} %all-gather.2.cloned.1.call-done, f32[2048,18992]{0,1:T(8,128)} %get-tuple-element.18, f32[2048]{0:T(1024)S(1)} %broadcast_divide_fusion, f32[2048]{0:T(1024)S(1)} %get-tuple-element.12, s32[2048]{0:T(1024)S(1)} %copy-done.6), kind=kOutput, calls=%fused_computation.19 | convolution fusion | flops 79893692416 | bytes 198696960 | tf_op jit(solution)/shard_map/tv,dv->td/dot_general | solution.py:30
  568.1 0.0 all-reduce.5.cloned.1.call-update
  568.1 0.0 copy-done.3
  568.2 0.0 copy-done.5
  568.2 110.5 %fusion.10 = f32[1024,18992]{0,1:T(8,128)} fusion(bf16[2048,1024]{1,0:T(8,128)(2,1)} %param.5, f32[1024]{0:T(1024)S(1)} %copy-done.5, f32[2048]{0:T(1024)S(1)} %copy-done.3, f32[2048,18992]{0,1:T(8,128)} %get-tuple-element.18, f32[2048]{0:T(1024)S(1)} %broadcast_divide_fusion, f32[2048]{0:T(1024)S(1)} %get-tuple-element.12, s32[2048]{0:T(1024)S(1)} %copy-done.6), kind=kOutput, calls=%fused_computation.20 | convolution fusion | flops 79899983872 | bytes 237604864 | tf_op jit(solution)/shard_map/td,tv->dv/dot_general | solution.py:35
  680.0 39.6 %all-reduce.5.cloned.1.call-done = bf16[2048,1024]{1,0:T(8,128)(2,1)} async-done(((bf16[2048,1024]{1,0:T(8,128)(2,1)}), bf16[2048,1024]{1,0:T(8,128)(2,1)}) %all-reduce.5.cloned.1.call-update) | async-done | bytes 4194320 | tf_op jit(solution)/shard_map/psum | solution.py:31
  719.6 5.1 fusion.9
  724.7 1306.4 %all-reduce.6 = (bf16[1024,18992]{0,1:T(8,128)(2,1)}, f32[1024]{0:T(1024)}) all-reduce(f32[1024,18992]{0,1:T(8,128)} %fusion.10, f32[1024]{0:T(1024)S(1)} %get-tuple-element.6), channel_id=2, replica_groups=mesh['tp'=8,'fsdp'=4] {'fsdp'}, use_global_device_ids=true, to_apply=%region_11.12.clone | all-reduce | flops 19448832 | bytes 116695040
  2031.1 0.0 copy-start
  2031.1 0.0 copy-start.1
  2031.1 10.7 dynamic-slice_convert_fusion
  2041.8 0.0 copy-done
  2041.8 0.0 copy-done.1
  2041.8 3.5 fusion.5
  (5 shorter events, 0.1 us)
Async XLA Ops:
  7.2 0.9 copy-start.10
  7.2 0.8 copy-start.9
  7.2 4.6 copy-start.8
  7.2 244.3 %all-gather.2.cloned.1.call-start = ((), (), s32[]{:S(2)}) async-start(), calls=%async_computation | async-start | bytes 48619520 | tf_op jit(solution)/shard_map/all_gather | solution.py:11
  7.9 711.7 %all-reduce.5.cloned.1.call-start = ((), (), s32[]{:S(2)}) async-start(), calls=%async_computation.1 | async-start | bytes 8388608 | tf_op jit(solution)/shard_map/psum | solution.py:31
  8.0 337.1 %copy-start.4 = (f32[1024]{0:T(1024)}, f32[1024]{0:T(1024)S(1)}, u32[]{:S(2)}) copy-start(f32[1024]{0:T(1024)S(1)} %convert_element_type.28) | copy-start | bytes 12292
  11.8 333.3 %copy-start.2 = (f32[2048]{0:T(1024)}, f32[2048]{0:T(1024)S(1)}, u32[]{:S(2)}) copy-start(f32[2048]{0:T(1024)S(1)} %add_rsqrt_fusion) | copy-start | bytes 24580
  251.5 115.2 %copy-start.6 = (s32[2048]{0:T(1024)S(1)}, s32[2048]{0:T(1024)}, u32[]{:S(2)}) copy-start(s32[2048]{0:T(1024)} %broadcast_subtract_fusion) | copy-start | bytes 24580
  366.7 80.8 %copy-start.7 = (f32[2048]{0:T(1024)S(1)}, f32[2048]{0:T(1024)}, u32[]{:S(2)}) copy-start(f32[2048]{0:T(1024)} %param.7) | copy-start | bytes 24580
  457.6 110.6 %copy-start.3 = (f32[2048]{0:T(1024)S(1)}, f32[2048]{0:T(1024)}, u32[]{:S(2)}) copy-start(f32[2048]{0:T(1024)} %copy-done.2) | copy-start | bytes 24580
  457.6 110.6 %copy-start.5 = (f32[1024]{0:T(1024)S(1)}, f32[1024]{0:T(1024)}, u32[]{:S(2)}) copy-start(f32[1024]{0:T(1024)} %copy-done.4) | copy-start | bytes 12292
  2031.1 10.7 copy-start
  2031.1 10.7 copy-start.1
Sparse Core Ops, SparseCore 0:
  9.6 241.8 all-gather.1
  568.3 151.3 all-reduce.4
where the time goes:
time: 2050 us
  blocking collectives  1370 us (67%)
  matrix products  315 us (15%)
  waiting for transfers between devices  279 us (14%)
  other arithmetic  62.6 us (3%)
    unnamed x1, blocking collectives  1310 us
    all_gather x1, waiting for transfers between devices, per_device(): w_cols = lax.all_gather(w_rows, 'fsdp', axis=0, tiled=True)  239 us
    dot_general x1, matrix products, per_device(): jnp.einsum('tv,dv->td', d_logits, w_cols, preferred_element_type=jnp.floa...  111 us
    dot_general x1, matrix products, per_device(): jnp.einsum('td,tv->dv', z_rows, d_logits, preferred_element_type=jnp.floa...  111 us
    dot_general x1, matrix products, per_device(): logits = jnp.dot(z_rows, w_cols, preferred_element_type=jnp.float32)  93.6 us
    reduce_sum x1, other arithmetic, per_device(): jnp.sum(jnp.exp(logits - row_max[:, None]), axis=1)  47.7 us
  transfers between devices with their start and end apart: 2, of which 2 were waited for; matrix products, arithmetic and copies ran while one was open for 6% of the time, Pallas kernels for 0%

commit v1 on v0

v1 whole, which is shorter than its diff:
```python
import functools

import jax
import jax.numpy as jnp
from jax import lax
from jax.experimental import pallas as pl
from jax.experimental.pallas import tpu as pltpu
from jax.sharding import PartitionSpec as P

NORM_EPS = 1e-6
LOG2E = 1.4426950408889634
NEG = -1e30
CHUNK = 512
TOK = 2048
TOK_DZ = 256
Z_ROWS = 512
AHEAD = 5
VMEM_LIMIT = 63 * 1024 * 1024
MESH = pl.DeviceIdType.MESH
f32, bf16 = jnp.float32, jnp.bfloat16


def dot_nt(a, b):
    return lax.dot_general(a, b, (((1,), (1,)), ((), ())), preferred_element_type=f32)


def dot_tn(a, b):
    return lax.dot_general(a, b, (((0,), (0,)), ((), ())), preferred_element_type=f32)


def dot_nn(a, b):
    return lax.dot_general(a, b, (((1,), (0,)), ((), ())), preferred_element_type=f32)


def cols(k, size):
    return pl.ds(pl.multiple_of(k * size, size), size)


class Sizes:
    def __init__(self, vocab_tp, n_fsdp, chunk):
        self.n = n_fsdp
        self.rows = -(-vocab_tp // (n_fsdp * 16)) * 16
        self.short = n_fsdp * self.rows - vocab_tp
        self.full = self.rows // chunk
        self.rem = self.rows - self.full * chunk
        self.solid = self.rem - self.short
        assert self.rem > self.short and self.rem % 16 == 0 and self.short % 16 == 0


def logits_kernel(sz, chunk, tok, h_hbm, w_hbm, gain, lab, l_hbm, z_hbm, wb_hbm, stat, z, w, lb0, lb1, hb0, hb1, m, s, hit, send, recv, loc, hsem, lsem, osem):
    me = lax.axis_index('fsdp')
    n, width = sz.n, w_hbm.shape[1]
    tokens = h_hbm.shape[0]
    lbufs, hbufs = (lb0, lb1), (hb0, hb1)

    barrier = pltpu.get_barrier_semaphore()
    for k in range(1, n):
        pl.semaphore_signal(barrier, inc=1, device_id={'fsdp': lax.rem(me + k, n)}, device_id_type=MESH)
    pl.semaphore_wait(barrier, n - 1)

    def remote(k, c, row0, rows):
        dest = lax.rem(me + k, n)
        return pltpu.make_async_remote_copy(
            src_ref=w_hbm.at[pl.ds(pl.multiple_of(dest * sz.rows + row0, 16), rows), :],
            dst_ref=w.at[pl.ds(pl.multiple_of(row0, 16), rows), cols(me, width)],
            send_sem=send.at[c, k], recv_sem=recv.at[c, k], device_id={'fsdp': dest}, device_id_type=MESH)

    def arrival(k, c, row0, rows):
        src = lax.rem(me + n - k, n)
        return pltpu.make_async_remote_copy(
            src_ref=w_hbm.at[pl.ds(0, rows), :],
            dst_ref=w.at[pl.ds(pl.multiple_of(row0, 16), rows), cols(src, width)],
            send_sem=send.at[c, k], recv_sem=recv.at[c, k], device_id={'fsdp': src}, device_id_type=MESH)

    def local(c, row0, rows):
        return pltpu.make_async_copy(
            w_hbm.at[pl.ds(pl.multiple_of(me * sz.rows + row0, 16), rows), :],
            w.at[pl.ds(pl.multiple_of(row0, 16), rows), cols(me, width)], loc.at[c])

    row_rem = sz.full * chunk
    row_odd = row_rem + sz.solid

    def issue(c):
        local(c, c * chunk, chunk).start()
        for k in range(1, n):
            remote(k, c, c * chunk, chunk).start()

    def when_not_last(dest, fn):
        if sz.short:
            pl.when(dest != n - 1)(fn)

    def issue_rem():
        local(sz.full, row_rem, sz.solid).start()
        when_not_last(me, lambda: local(sz.full + 1, row_odd, sz.short).start())
        for k in range(1, n):
            remote(k, sz.full, row_rem, sz.solid).start()
            when_not_last(lax.rem(me + k, n), lambda: remote(k, sz.full + 1, row_odd, sz.short).start())

    ahead = min(AHEAD, sz.full)
    for c in range(ahead):
        issue(c)

    if sz.short:
        @pl.when(me == n - 1)
        def _():
            w[row_odd:, :] = jnp.zeros((sz.short, w.shape[1]), bf16)

    z_rows = hb0.shape[0]
    n_z = tokens // z_rows

    def load_h(i, b):
        return pltpu.make_async_copy(h_hbm.at[cols(i, z_rows), :], hbufs[b], hsem.at[b])

    load_h(0, 0).start()
    load_h(1, 1).start()

    def norm(i, _):
        for b in (0, 1):
            k = 2 * i + b
            load_h(k, b).wait()
            h = hbufs[b][...].astype(f32)
            inv = lax.rsqrt(jnp.mean(h * h, axis=-1, keepdims=True) + NORM_EPS)
            z[cols(k, z_rows), :] = (h * inv * gain[...].astype(f32)).astype(bf16)

            @pl.when(k + 2 < n_z)
            def _():
                load_h(k + 2, b).start()
        return 0

    lax.fori_loop(0, n_z // 2, norm, 0)
    z_out = pltpu.make_async_copy(z, z_hbm, osem.at[0])
    z_out.start()

    m[...] = jnp.full(m.shape, NEG, f32)
    s[...] = jnp.zeros(s.shape, f32)
    hit[...] = jnp.zeros(hit.shape, f32)
    n_tok = tokens // tok
    sub = min(256, tok)
    lane = min(128, sub)

    def out_copy(row0, rows, k, b):
        return pltpu.make_async_copy(lbufs[b].at[pl.ds(0, rows), :], l_hbm.at[pl.ds(pl.multiple_of(row0, 16), rows), cols(k, tok)], lsem.at[b])

    def tile(row0, rows, k, b, masked):
        group = min(4, rows // 8)
        sub_rows = lax.broadcasted_iota(jnp.int32, (8, lane), 0)
        for c0 in range(0, tok, sub):
            logits = dot_nt(w[pl.ds(pl.multiple_of(row0, 16), rows), :], z[pl.ds(pl.multiple_of(k * tok + c0, sub), sub), :]) * LOG2E
            if masked:
                ids = lax.broadcasted_iota(jnp.int32, (rows, sub), 0)
                logits = jnp.where(ids < jnp.where(me == n - 1, sz.solid, sz.rem), logits, NEG)
            lbufs[b][0:rows, c0:c0 + sub] = logits
            for c1 in range(0, sub, lane):
                sl = pl.ds(pl.multiple_of(k * tok + c0 + c1, lane), lane)
                big, tot, got = m[:, sl], s[:, sl], hit[:, sl]
                rel = lab[0:1, sl] - row0 - sub_rows
                for g in range(0, rows // 8, group):
                    part = [logits[8 * r:8 * r + 8, c1:c1 + lane] for r in range(g, min(g + group, rows // 8))]
                    new = functools.reduce(jnp.maximum, part, big)
                    tot = tot * jnp.exp2(big - new)
                    for r, x in enumerate(part):
                        tot += jnp.exp2(x - new)
                        got += jnp.where(rel == 8 * (g + r), x, 0.0)
                    big = new
                m[:, sl], s[:, sl], hit[:, sl] = big, tot, got

    def chunk_rows(row0, rows, first, masked):
        def step(i, _):
            for b in (0, 1):
                k = 2 * i + b

                @pl.when(jnp.logical_not(jnp.logical_and(first, i == 0)))
                def _():
                    out_copy(0, chunk if not masked else rows, 0, b).wait()
                tile(row0, rows, k, b, masked)
                out_copy(row0, rows, k, b).start()
            return 0
        lax.fori_loop(0, n_tok // 2, step, 0)

    def full_chunk(c, _):
        local(c, c * chunk, chunk).wait()
        for k in range(1, n):
            arrival(k, c, c * chunk, chunk).wait_recv()

        @pl.when(c + ahead < sz.full)
        def _():
            issue(c + ahead)

        @pl.when(c + ahead == sz.full)
        def _():
            issue_rem()
        chunk_rows(c * chunk, chunk, c == 0, False)
        return 0

    lax.fori_loop(0, sz.full, full_chunk, 0)
    for b in (0, 1):
        out_copy(0, chunk, 0, b).wait()
    local(sz.full, row_rem, sz.solid).wait()
    when_not_last(me, lambda: local(sz.full + 1, row_odd, sz.short).wait())
    for k in range(1, n):
        arrival(k, sz.full, row_rem, sz.solid).wait_recv()
        when_not_last(me, lambda: arrival(k, sz.full + 1, row_odd, sz.short).wait_recv())
    w_out = pltpu.make_async_copy(w, wb_hbm, osem.at[1])
    w_out.start()
    chunk_rows(row_rem, sz.rem, True, True)
    for b in (0, 1):
        out_copy(0, sz.rem, 0, b).wait()

    big = jnp.max(m[...], axis=0, keepdims=True)
    stat[0:1, :] = big
    stat[1:2, :] = jnp.sum(s[...] * jnp.exp2(m[...] - big), axis=0, keepdims=True)
    stat[2:3, :] = jnp.sum(hit[...], axis=0, keepdims=True)
    z_out.wait()
    w_out.wait()

    def drain(c, _):
        for k in range(1, n):
            remote(k, c, c * chunk, chunk).wait_send()
        return 0

    lax.fori_loop(0, sz.full, drain, 0)
    for k in range(1, n):
        remote(k, sz.full, row_rem, sz.solid).wait_send()
        when_not_last(lax.rem(me + k, n), lambda: remote(k, sz.full + 1, row_odd, sz.short).wait_send())


def head_grad_kernel(sz, chunk, tok, z_hbm, l_hbm, st, lab, g_hbm, dw_hbm, z, l0, l1, g0, g1, acc, stage, zsem, lsem, gsem, dsem):
    tokens = z_hbm.shape[0]
    lbufs, gbufs = (l0, l1), (g0, g1)
    n_tok = tokens // tok
    lane = min(128, tok)
    z_in = pltpu.make_async_copy(z_hbm, z, zsem.at[0])
    z_in.start()

    def load(row0, rows, k, b):
        return pltpu.make_async_copy(l_hbm.at[pl.ds(pl.multiple_of(row0, 16), rows), cols(k, tok)], lbufs[b].at[pl.ds(0, rows), :], lsem.at[b])

    def save(row0, rows, k, b):
        return pltpu.make_async_copy(gbufs[b].at[pl.ds(0, rows), :], g_hbm.at[pl.ds(pl.multiple_of(row0, 16), rows), cols(k, tok)], gsem.at[b])

    def put(row0, rows):
        return pltpu.make_async_copy(stage.at[pl.ds(0, rows), :], dw_hbm.at[pl.ds(pl.multiple_of(row0, 16), rows), :], dsem.at[0])

    acc[...] = jnp.zeros(acc.shape, f32)

    def tile(row0, rows, k, b):
        ids = lax.broadcasted_iota(jnp.int32, (rows, lane), 0)
        step = min(256, tok)
        total = None
        for c0 in range(0, tok, step):
            for c1 in range(c0, c0 + step, lane):
                sl = pl.ds(pl.multiple_of(k * tok + c1, lane), lane)
                p = jnp.exp2(lbufs[b][0:rows, c1:c1 + lane] - st[0:1, sl])
                g = jnp.where(ids == lab[0:1, sl] - row0, p - 1.0, p) * st[1:2, sl]
                gbufs[b][0:rows, c1:c1 + lane] = g.astype(bf16)
            d = dot_nn(gbufs[b][0:rows, c0:c0 + step], z[pl.ds(pl.multiple_of(k * tok + c0, step), step), :])
            total = d if total is None else total + d
        acc[0:rows, :] += total

    def chunk_rows(row0, rows, first, next_row0, next_rows, has_next):
        def step(i, _):
            for b in (0, 1):
                k = 2 * i + b
                load(row0, rows, k, b).wait()

                @pl.when(jnp.logical_not(jnp.logical_and(first, i == 0)))
                def _():
                    save(row0, rows, 0, b).wait()
                tile(row0, rows, k, b)
                save(row0, rows, k, b).start()

                @pl.when(k + 2 < n_tok)
                def _():
                    load(row0, rows, k + 2, b).start()
            return 0
        lax.fori_loop(0, n_tok // 2, step, 0)

    for b in (0, 1):
        load(0, chunk, b, b).start()
    z_in.wait()

    def full_chunk(c, _):
        chunk_rows(c * chunk, chunk, c == 0, None, None, None)

        @pl.when(c + 1 < sz.full)
        def _():
            for b in (0, 1):
                load((c + 1) * chunk, chunk, b, b).start()

        @pl.when(c + 1 == sz.full)
        def _():
            for b in (0, 1):
                load(sz.full * chunk, sz.rem, b, b).start()

        @pl.when(c > 0)
        def _():
            put(0, chunk).wait()
        stage[...] = acc[...].astype(bf16)
        acc[...] = jnp.zeros(acc.shape, f32)
        put(c * chunk, chunk).start()
        return 0

    lax.fori_loop(0, sz.full, full_chunk, 0)
    for b in (0, 1):
        save(0, chunk, 0, b).wait()
    put(0, chunk).wait()
    chunk_rows(sz.full * chunk, sz.rem, True, None, None, None)
    for b in (0, 1):
        save(0, sz.rem, 0, b).wait()
    stage[0:sz.rem, :] = acc[0:sz.rem, :].astype(bf16)
    last = put(sz.full * chunk, sz.rem)
    last.start()
    last.wait()


def dz_kernel(tok, w_hbm, g_hbm, o_hbm, w, g0, g1, o0, o1, wsem, gsem, osem):
    gbufs, obufs = (g0, g1), (o0, o1)
    n_tok = g_hbm.shape[1] // tok
    w_in = pltpu.make_async_copy(w_hbm, w, wsem.at[0])
    w_in.start()

    def load(k, b):
        return pltpu.make_async_copy(g_hbm.at[:, cols(k, tok)], gbufs[b], gsem.at[b])

    def put(k, b):
        return pltpu.make_async_copy(obufs[b], o_hbm.at[cols(k, tok), :], osem.at[b])

    for b in (0, 1):
        load(b, b).start()
    w_in.wait()

    def step(i, _):
        for b in (0, 1):
            k = 2 * i + b
            load(k, b).wait()

            @pl.when(i > 0)
            def _():
                put(0, b).wait()
            obufs[b][...] = dot_tn(gbufs[b][...], w[...]).astype(bf16)
            put(k, b).start()

            @pl.when(k + 2 < n_tok)
            def _():
                load(k + 2, b).start()
        return 0

    lax.fori_loop(0, n_tok // 2, step, 0)
    for b in (0, 1):
        put(0, b).wait()


HBM = pl.BlockSpec(memory_space=pl.ANY)
VM = pl.BlockSpec(memory_space=pltpu.VMEM)
DMA = pltpu.SemaphoreType.DMA


def params(**kw):
    return pltpu.CompilerParams(vmem_limit_bytes=VMEM_LIMIT, **kw)


def solution(mesh, chunk=CHUNK, tok=TOK, tok_dz=TOK_DZ, z_rows=Z_ROWS):
    n_fsdp, n_tp = mesh.shape['fsdp'], mesh.shape['tp']
    everyone = ('fsdp', 'tp')
    S = jax.ShapeDtypeStruct

    def per_device(hidden, labels, tok_mask, norm_gain, w_rows):
        fsdp_id, tp_id = lax.axis_index('fsdp'), lax.axis_index('tp')
        d = hidden.shape[1]
        width, vocab_tp = w_rows.shape
        tokens = hidden.shape[0] * n_fsdp
        sz = Sizes(vocab_tp, n_fsdp, chunk)
        rows_own = hidden.shape[0] // n_tp
        hid_own = lax.dynamic_slice_in_dim(hidden, tp_id * rows_own, rows_own, 0)
        hid_all = lax.all_gather(hid_own, everyone, axis=0, tiled=True)
        lab_all = lax.all_gather(labels, 'fsdp', axis=0, tiled=True)
        mask_all = lax.all_gather(tok_mask, 'fsdp', axis=0, tiled=True)
        gain_f32 = norm_gain.astype(f32)
        mine = lab_all // vocab_tp == tp_id
        lab_loc = jnp.where(mine, lab_all - tp_id * vocab_tp - fsdp_id * sz.rows, -1)[None, :]

        logits, z_all, w_blk, stats = pl.pallas_call(
            functools.partial(logits_kernel, sz, chunk, tok),
            out_shape=(S((sz.rows, tokens), f32), S((tokens, d), bf16), S((sz.rows, d), bf16), S((8, tokens), f32)),
            in_specs=[HBM, HBM, VM, VM], out_specs=(HBM, HBM, HBM, VM),
            scratch_shapes=[pltpu.VMEM((tokens, d), bf16), pltpu.VMEM((sz.rows, d), bf16), pltpu.VMEM((chunk, tok), f32), pltpu.VMEM((chunk, tok), f32),
                            pltpu.VMEM((z_rows, d), bf16), pltpu.VMEM((z_rows, d), bf16),
                            pltpu.VMEM((8, tokens), f32), pltpu.VMEM((8, tokens), f32), pltpu.VMEM((8, tokens), f32),
                            DMA((sz.full + 2, n_fsdp)), DMA((sz.full + 2, n_fsdp)), DMA((sz.full + 2,)), DMA((2,)), DMA((2,)), DMA((2,))],
            compiler_params=params(collective_id=0, has_side_effects=True), name='logits',
        )(hid_all, w_rows.T, norm_gain[None, :], lab_loc)

        big = lax.pmax(stats[0], everyone)
        tot = lax.psum(jnp.stack([stats[1] * jnp.exp2(stats[0] - big), stats[2]]), everyone)
        lse = big + jnp.log2(tot[0])
        count = jnp.sum(mask_all)
        mean_loss = jnp.sum(mask_all * (lse - tot[1])) / LOG2E / count
        st = jnp.stack([lse, mask_all / count])

        g_t, dw_t = pl.pallas_call(
            functools.partial(head_grad_kernel, sz, chunk, tok),
            out_shape=(S((sz.rows, tokens), bf16), S((sz.rows, d), bf16)),
            in_specs=[HBM, HBM, VM, VM], out_specs=(HBM, HBM),
            scratch_shapes=[pltpu.VMEM((tokens, d), bf16), pltpu.VMEM((chunk, tok), f32), pltpu.VMEM((chunk, tok), f32), pltpu.VMEM((chunk, tok), bf16), pltpu.VMEM((chunk, tok), bf16),
                            pltpu.VMEM((chunk, d), f32), pltpu.VMEM((chunk, d), bf16), DMA((1,)), DMA((2,)), DMA((2,)), DMA((1,))],
            compiler_params=params(), name='head_grad',
        )(z_all, logits, st, lab_loc)

        grad_part = pl.pallas_call(
            functools.partial(dz_kernel, tok_dz),
            out_shape=S((tokens, d), bf16), in_specs=[HBM, HBM], out_specs=HBM,
            scratch_shapes=[pltpu.VMEM((sz.rows, d), bf16), pltpu.VMEM((sz.rows, tok_dz), bf16), pltpu.VMEM((sz.rows, tok_dz), bf16),
                            pltpu.VMEM((tok_dz, d), bf16), pltpu.VMEM((tok_dz, d), bf16), DMA((1,)), DMA((2,)), DMA((2,))],
            compiler_params=params(), name='dz',
        )(w_blk, g_t)

        grad_z = lax.psum_scatter(grad_part, 'fsdp', scatter_dimension=0, tiled=True)
        grad_z = lax.psum_scatter(grad_z, 'tp', scatter_dimension=0, tiled=True).astype(f32)
        hid_f32 = hid_own.astype(f32)
        inv_rms = lax.rsqrt(jnp.mean(hid_f32 * hid_f32, axis=-1, keepdims=True) + NORM_EPS)
        normed = hid_f32 * inv_rms
        d_normed = grad_z * gain_f32
        grad_hid = inv_rms * (d_normed - normed * jnp.mean(d_normed * normed, axis=-1, keepdims=True))
        grad_hidden = lax.all_gather(grad_hid.astype(bf16), 'tp', axis=0, tiled=True)
        grad_gain = lax.psum(jnp.sum(grad_z * normed, axis=0), everyone)
        grad_head = lax.all_to_all(dw_t, 'fsdp', split_axis=1, concat_axis=0, tiled=True)
        return mean_loss, grad_hidden, grad_head[:vocab_tp].T, grad_gain

    return jax.shard_map(per_device, mesh=mesh, in_specs=(P('fsdp', None), P('fsdp'), P('fsdp'), P(), P('fsdp', 'tp')), out_specs=(P(), P('fsdp', None), P('fsdp', 'tp'), P()), check_vma=False)
```

time: 2050 us -> 959 us (0.47)
  blocking collectives: 1370 us -> 93.9 us
  Pallas kernels: 0 us -> 348 us
  matrix products: 315 us -> 0 us
  waiting for transfers between devices: 279 us -> 458 us
  other arithmetic: 62.6 us -> 9.88 us
    unnamed x1 -> x0, blocking collectives: 1310 us -> none
    pallas_call x0 -> x3, Pallas kernels: none -> 348 us  [the longest x1 129 us: per_device(): pl.pallas_call(functools.partial(head_grad_kernel, sz, chunk, tok), out_s...]
    dot_general x3 -> x0, matrix products: 315 us -> none  [the longest x1 111 us: per_device(): jnp.einsum('tv,dv->td', d_logits, w_cols, preferred_element_type=jnp.floa...]
    reduce_scatter x0 -> x2, waiting for transfers between devices: none -> 201 us  [the longest x1 123 us: per_device(): lax.psum_scatter(grad_part, 'fsdp', scatter_dimension=0, tiled=True)]
    all_gather x1 -> x2, waiting for transfers between devices: 239 us -> 111 us  [the longest x1 111 us: per_device(): hid_all = lax.all_gather(hid_own, everyone, axis=0, tiled=True)]
    psum x1, waiting for transfers between devices: 39.6 us -> 122 us  [per_device(): lax.psum(jnp.stack([stats[1] * jnp.exp2(stats[0] - big), stats[2]]), ever...]
    reduce_sum x4 -> x3, other arithmetic: 56.5 us -> 4.06 us  [the longest x1 1.93 us: per_device(): jnp.mean(hid_f32 * hid_f32, axis=-1, keepdims=True) + NORM_EPS]
    all_to_all x0 -> x1, waiting for transfers between devices: none -> 24.4 us  [per_device(): lax.all_to_all(dw_t, 'fsdp', split_axis=1, concat_axis=0, tiled=True)]
  transfers between devices with their start and end apart: 2 -> 6, of which waited for: 2 -> 5; matrix products, arithmetic and copies ran while one was open for 6% -> 2% of each run, Pallas kernels for 0% -> 0%
where the time goes in v1:
time: 959 us; the launch traced here: 957 us
  waiting for transfers between devices  458 us (48%)
  Pallas kernels  348 us (36%)
  blocking collectives  93.9 us (10%)
  local copies, waits for them, and re-layouts  24.6 us (3%)
  between operations  16.3 us (2%)
  other arithmetic  9.88 us (1%)
    pallas_call x1, Pallas kernels, per_device(): pl.pallas_call(functools.partial(head_grad_kernel, sz, chunk, tok), out_s...  129 us
    pallas_call x1, Pallas kernels, per_device(): pl.pallas_call(functools.partial(logits_kernel, sz, chunk, tok), out_shap...  125 us
    reduce_scatter x1, waiting for transfers between devices, per_device(): lax.psum_scatter(grad_part, 'fsdp', scatter_dimension=0, tiled=True)  123 us
    psum x1, waiting for transfers between devices, per_device(): lax.psum(jnp.stack([stats[1] * jnp.exp2(stats[0] - big), stats[2]]), ever...  122 us
    all_gather x1, waiting for transfers between devices, per_device(): hid_all = lax.all_gather(hid_own, everyone, axis=0, tiled=True)  111 us
    pallas_call x1, Pallas kernels, per_device(): pl.pallas_call(functools.partial(dz_kernel, tok_dz), out_shape=S((tokens,...  93.9 us
    reduce_scatter x1, waiting for transfers between devices, per_device(): lax.psum_scatter(grad_z, 'tp', scatter_dimension=0, tiled=True).astype(f32)  77.7 us
    pmax x1, blocking collectives, per_device(): big = lax.pmax(stats[0], everyone)  41.1 us
  transfers between devices with their start and end apart: 6, of which 5 were waited for; matrix products, arithmetic and copies ran while one was open for 2% of the time, Pallas kernels for 0%

profile of v1, /device:TPU:0, one launch (start us, length us, event | category | flops | bytes accessed | tf_op | source)
XLA Modules:
  0.0 957.3 jit_solution(17811080255612654278)
XLA Ops:
  7.2 0.0 all-gather.3.cloned.1.call-start
  7.2 1.9 fusion.6
  9.1 0.0 all-gather.3.cloned.1.call-update
  9.2 0.0 all-reduce.2.cloned.1.call-start
  9.2 1.3 broadcast_in_dim.6.gain
  10.5 6.2 all_gather.14
  16.7 0.6 subtract_select_fusion
  17.3 111.2 %all-gather.3.cloned.1.call-done.h_hbm = bf16[8192,1024]{1,0:T(8,128)(2,1)} async-done(((bf16[256,1024]{1,0:T(8,128)(2,1)}), bf16[8192,1024]{1,0:T(8,128)(2,1)}) %all-gather.3.cloned.1.call-update) | async-done | bytes 16777232 | tf_op jit(solution)/shard_map/all_gather | solution.py:375
  128.6 0.0 copy-start.1
  128.6 125.1 %logits.1 = (f32[4752,8192]{1,0:T(8,128)}, bf16[8192,1024]{1,0:T(8,128)(2,1)}, bf16[4752,1024]{1,0:T(8,128)(2,1)}, f32[8,8192]{1,0:T(8,128)}) custom-call(bf16[8192,1024]{1,0:T(8,128)(2,1)} %all-gather.3.cloned.1.call-done.h_hbm, bf16[18992,256]{1,0:T(8,128)(2,1)} %bitcast.20, bf16[1,1024]{1,0:T(2,128)(2,1)} %broadcast_in_dim.6.gain, s32[1,8192]{1,0:T(1,128)} %bitcast.23), custom_call_target="tpu_custom_call" | custom-call | tf_op jit(solution)/shard_map/logits/pallas_call | solution.py:382
  253.7 1.2 fusion.12
  254.9 41.1 %pmax.7 = f32[8192]{0:T(1024)S(1)} all-reduce(f32[8192]{0:T(1024)S(1)} %bitcast.21), channel_id=1, replica_groups=mesh['tp'=8,'fsdp'=4] {'fsdp','tp'}, use_global_device_ids=true, to_apply=%region_0.1 | all-reduce | flops 8192 | bytes 65536 | tf_op jit(solution)/shard_map/pmax | solution.py:393
  296.1 0.7 pad_maximum_fusion
  296.8 0.0 all-reduce.2.cloned.1.call-update
  296.8 0.0 reduce-scatter.3.cloned.1.call-start
  296.8 0.0 copy-done.1
  296.9 5.6 all_gather.12
  302.5 121.6 %all-reduce.2.cloned.1.call-done = f32[2,8192]{1,0:T(2,128)} async-done(((f32[2,8192]{1,0:T(2,128)}), f32[2,8192]{1,0:T(2,128)}) %all-reduce.2.cloned.1.call-update) | async-done | bytes 65552 | tf_op jit(solution)/shard_map/psum | solution.py:394
  424.1 1.0 fusion.9
  425.1 0.6 fusion.11
  425.7 0.7 broadcast_divide_fusion
  426.4 0.7 pad_maximum_fusion.1.st
  427.1 129.0 %head_grad.1 = (bf16[4752,8192]{1,0:T(8,128)(2,1)}, bf16[4752,1024]{1,0:T(8,128)(2,1)}) custom-call(bf16[8192,1024]{1,0:T(8,128)(2,1)} %get-tuple-element.12.z_hbm, f32[4752,8192]{1,0:T(8,128)} %get-tuple-element.13.l_hbm, f32[2,8192]{1,0:T(2,128)} %pad_maximum_fusion.1.st, s32[1,8192]{1,0:T(1,128)} %bitcast.24), custom_call_target="tpu_custom_call" | custom-call | tf_op jit(solution)/shard_map/head_grad/pallas_call | solution.py:400
  556.0 93.9 %dz.1 = bf16[8192,1024]{1,0:T(8,128)(2,1)} custom-call(bf16[4752,1024]{1,0:T(8,128)(2,1)} %get-tuple-element.11.w_hbm, bf16[4752,8192]{1,0:T(8,128)(2,1)} %get-tuple-element.14.g_hbm), custom_call_target="tpu_custom_call" | custom-call | tf_op jit(solution)/shard_map/dz/pallas_call | solution.py:409
  649.9 0.0 reduce-scatter.3.cloned.1.call-update
  650.0 0.0 reduce-scatter.5.cloned.1.call-start
  650.0 123.4 %reduce-scatter.3.cloned.1.call-done = bf16[2048,1024]{1,0:T(8,128)(2,1)} async-done(((bf16[8192,1024]{1,0:T(8,128)(2,1)}), bf16[2048,1024]{1,0:T(8,128)(2,1)}) %reduce-scatter.3.cloned.1.call-update) | async-done | bytes 4194320 | tf_op jit(solution)/shard_map/reduce_scatter | solution.py:417
  773.4 0.0 reduce-scatter.5.cloned.1.call-update
  773.5 8.1 copy.13
  781.6 0.0 copy-start.2
  781.6 0.0 copy-start
  781.6 6.0 all-to-all-start
  787.6 0.0 all-gather.5.cloned.1.call-start
  787.6 0.0 copy-done.2
  787.6 77.7 %reduce-scatter.5.cloned.1.call-done = bf16[256,1024]{1,0:T(8,128)(2,1)} async-done(((bf16[2048,1024]{1,0:T(8,128)(2,1)}), bf16[256,1024]{1,0:T(8,128)(2,1)}) %reduce-scatter.5.cloned.1.call-update) | async-done | bytes 524304 | tf_op jit(solution)/shard_map/reduce_scatter | solution.py:418
  865.3 0.0 copy-done
  865.3 1.5 fusion.7
  866.9 2.1 fusion.4
  869.0 0.0 all-gather.5.cloned.1.call-update
  870.4 24.4 %all-to-all-done = bf16[4752,4,256]{2,0,1:T(8,128)(2,1)} async-done(((bf16[4752,4,256]{2,0,1:T(8,128)(2,1)}), bf16[4752,4,256]{2,0,1:T(8,128)(2,1)}, u32[]{:S(2)}, u32[]{:S(2)}) %all-to-all-start) | async-done | bytes 9732128 | tf_op jit(solution)/shard_map/all_to_all | solution.py:426
  894.8 9.3 slice_bitcast_fusion
  904.1 41.0 %psum.15 = f32[1024]{0:T(1024)} all-reduce(f32[1024]{0:T(1024)S(1)} %get-tuple-element.16), channel_id=1, replica_groups=mesh['tp'=8,'fsdp'=4] {'fsdp','tp'}, use_global_device_ids=true, to_apply=%region_9.10 | all-reduce | flops 1024 | bytes 8192 | tf_op jit(solution)/shard_map/psum | solution.py:425
  945.0 0.0 all-gather.5.cloned.1.call-done
  945.0 4.6 copy.16
  (4 shorter events, 0.0 us)
Async XLA Ops:
  7.2 121.4 %all-gather.3.cloned.1.call-start = ((), (), s32[]{:S(2)}) async-start(), calls=%async_computation.3 | async-start | bytes 17301504 | tf_op jit(solution)/shard_map/all_gather | solution.py:375
  9.2 414.9 %all-reduce.2.cloned.1.call-start = ((), (), s32[]{:S(2)}) async-start(), calls=%async_computation.4 | async-start | bytes 131072 | tf_op jit(solution)/shard_map/psum | solution.py:394
  128.6 168.3 %copy-start.1 = (f32[2048]{0:T(1024)S(1)}, f32[2048]{0:T(1024)}, u32[]{:S(2)}) copy-start(f32[2048]{0:T(1024)} %param.7) | copy-start | bytes 24580
  296.8 476.6 %reduce-scatter.3.cloned.1.call-start = ((), (), s32[]{:S(2)}) async-start(), calls=%async_computation.5 | async-start | bytes 20971520 | tf_op jit(solution)/shard_map/reduce_scatter | solution.py:417
  650.0 215.4 %reduce-scatter.5.cloned.1.call-start = ((), (), s32[]{:S(2)}) async-start(), calls=%async_computation.6 | async-start | bytes 4718592 | tf_op jit(solution)/shard_map/reduce_scatter | solution.py:418
  781.6 6.0 copy-start.2
  781.6 83.8 %copy-start = (bf16[256,1024]{1,0:T(8,128)(2,1)S(1)}, bf16[256,1024]{1,0:T(8,128)(2,1)}, u32[]{:S(2)}) copy-start(bf16[256,1024]{1,0:T(8,128)(2,1)} %get-tuple-element.21) | copy-start | bytes 1572868
  781.6 113.2 %all-to-all-start = ((bf16[4752,4,256]{2,0,1:T(8,128)(2,1)}), bf16[4752,4,256]{2,0,1:T(8,128)(2,1)}, u32[]{:S(2)}, u32[]{:S(2)}) async-start(bf16[4752,4,256]{2,0,1:T(8,128)(2,1)} %bitcast.18), calls=%async_computation.2 | async-start | bytes 19464192 | tf_op jit(solution)/shard_map/all_to_all | solution.py:426
  787.6 157.5 %all-gather.5.cloned.1.call-start = ((), (), s32[]{:S(2)}) async-start(), calls=%async_computation.7 | async-start | bytes 4718592 | tf_op jit(solution)/shard_map/all_gather | solution.py:424
Sparse Core Ops, SparseCore 0:
  11.6 116.8 all-gather.2
  296.9 127.1 all-reduce.1
  650.1 123.2 reduce-scatter.2
  776.9 88.3 reduce-scatter.4
  869.1 73.5 all-gather.4

commit v2 on v1

v2 whole, which is shorter than its diff:
```python
import functools

import jax
import jax.numpy as jnp
from jax import lax
from jax.experimental import pallas as pl
from jax.experimental.pallas import tpu as pltpu
from jax.sharding import PartitionSpec as P

NORM_EPS = 1e-6
LOG2E = 1.4426950408889634
NEG = -1e30
CHUNK = 512
TOK = 2048
EARLY = 6
Z_ROWS = 512
AHEAD = 5
VMEM_LIMIT = 67_043_328
MESH = pl.DeviceIdType.MESH
f32, bf16 = jnp.float32, jnp.bfloat16


def dot_nt(a, b):
    return lax.dot_general(a, b, (((1,), (1,)), ((), ())), preferred_element_type=f32)


def dot_tn(a, b):
    return lax.dot_general(a, b, (((0,), (0,)), ((), ())), preferred_element_type=f32)


def dot_nn(a, b):
    return lax.dot_general(a, b, (((1,), (0,)), ((), ())), preferred_element_type=f32)


def cols(k, size):
    return pl.ds(pl.multiple_of(k * size, size), size)


class Sizes:
    def __init__(self, vocab_tp, n_fsdp, chunk):
        self.n = n_fsdp
        self.rows = -(-vocab_tp // (n_fsdp * 16)) * 16
        self.short = n_fsdp * self.rows - vocab_tp
        self.full = self.rows // chunk
        self.rem = self.rows - self.full * chunk
        self.solid = self.rem - self.short
        assert self.rem > self.short and self.rem % 16 == 0 and self.short % 16 == 0


class Place:
    def __init__(self, n_fsdp, n_tp):
        self.n_fsdp, self.n_tp, self.n_all = n_fsdp, n_tp, n_fsdp * n_tp
        self.f, self.tp = lax.axis_index('fsdp'), lax.axis_index('tp')
        self.x, self.c = self.f // 2, lax.rem(self.f, 2)
        self.n_z = n_tp // 2
        self.z, self.y = self.tp // 2, lax.rem(self.tp, 2)
        self.index = self.tp * n_fsdp + self.f

    def other(self, k):
        i = lax.rem(self.index + k, self.n_all)
        return i // self.n_fsdp, lax.rem(i, self.n_fsdp)


def dev(tp, f):
    return {'tp': tp, 'fsdp': f}


def rcopy(src, dst, ssem, rsem, to):
    return pltpu.make_async_remote_copy(src_ref=src, dst_ref=dst, send_sem=ssem, recv_sem=rsem, device_id=to, device_id_type=MESH)


def enter(at):
    barrier = pltpu.get_barrier_semaphore()

    def tell(k, _):
        tp, f = at.other(k)
        pl.semaphore_signal(barrier, inc=1, device_id=dev(tp, f), device_id_type=MESH)
        return 0

    lax.fori_loop(1, at.n_all, tell, 0)
    pl.semaphore_wait(barrier, at.n_all - 1)


def logits_kernel(sz, n_tp, chunk, tok, h_hbm, w_hbm, gain, lab, scale, l_hbm, z_hbm, wb_hbm, st_out, z, w, lb0, lb1, hb0, hb1, m, s, hit, st_loc, got, res, st, send, recv, loc, hsem, lsem, osem, ssend, srecv, rsend, rrecv):
    at = Place(sz.n, n_tp)
    me = at.f
    n, width = sz.n, w_hbm.shape[1]
    tokens = h_hbm.shape[0]
    lbufs, hbufs = (lb0, lb1), (hb0, hb1)

    enter(at)

    def remote(k, c, row0, rows):
        dest = lax.rem(me + k, n)
        return pltpu.make_async_remote_copy(
            src_ref=w_hbm.at[pl.ds(pl.multiple_of(dest * sz.rows + row0, 16), rows), :],
            dst_ref=w.at[pl.ds(pl.multiple_of(row0, 16), rows), cols(me, width)],
            send_sem=send.at[c, k], recv_sem=recv.at[c, k], device_id={'fsdp': dest}, device_id_type=MESH)

    def arrival(k, c, row0, rows):
        src = lax.rem(me + n - k, n)
        return pltpu.make_async_remote_copy(
            src_ref=w_hbm.at[pl.ds(0, rows), :],
            dst_ref=w.at[pl.ds(pl.multiple_of(row0, 16), rows), cols(src, width)],
            send_sem=send.at[c, k], recv_sem=recv.at[c, k], device_id={'fsdp': src}, device_id_type=MESH)

    def local(c, row0, rows):
        return pltpu.make_async_copy(
            w_hbm.at[pl.ds(pl.multiple_of(me * sz.rows + row0, 16), rows), :],
            w.at[pl.ds(pl.multiple_of(row0, 16), rows), cols(me, width)], loc.at[c])

    row_rem = sz.full * chunk
    row_odd = row_rem + sz.solid

    def issue(c):
        local(c, c * chunk, chunk).start()
        for k in range(1, n):
            remote(k, c, c * chunk, chunk).start()

    def when_not_last(dest, fn):
        if sz.short:
            pl.when(dest != n - 1)(fn)

    def issue_rem():
        local(sz.full, row_rem, sz.solid).start()
        when_not_last(me, lambda: local(sz.full + 1, row_odd, sz.short).start())
        for k in range(1, n):
            remote(k, sz.full, row_rem, sz.solid).start()
            when_not_last(lax.rem(me + k, n), lambda: remote(k, sz.full + 1, row_odd, sz.short).start())

    ahead = min(AHEAD, sz.full)
    for c in range(ahead):
        issue(c)

    if sz.short:
        @pl.when(me == n - 1)
        def _():
            w[row_odd:, :] = jnp.zeros((sz.short, w.shape[1]), bf16)

    z_rows = hb0.shape[0]
    n_z = tokens // z_rows

    def load_h(i, b):
        return pltpu.make_async_copy(h_hbm.at[cols(i, z_rows), :], hbufs[b], hsem.at[b])

    load_h(0, 0).start()
    load_h(1, 1).start()

    def norm(i, _):
        for b in (0, 1):
            k = 2 * i + b
            load_h(k, b).wait()
            h = hbufs[b][...].astype(f32)
            inv = lax.rsqrt(jnp.mean(h * h, axis=-1, keepdims=True) + NORM_EPS)
            z[cols(k, z_rows), :] = (h * inv * gain[...].astype(f32)).astype(bf16)

            @pl.when(k + 2 < n_z)
            def _():
                load_h(k + 2, b).start()
        return 0

    lax.fori_loop(0, n_z // 2, norm, 0)
    z_out = pltpu.make_async_copy(z, z_hbm, osem.at[0])
    z_out.start()

    m[...] = jnp.full(m.shape, NEG, f32)
    s[...] = jnp.zeros(s.shape, f32)
    hit[...] = jnp.zeros(hit.shape, f32)
    n_tok = tokens // tok
    sub = min(256, tok)
    lane = min(128, sub)

    def out_copy(row0, rows, k, b):
        return pltpu.make_async_copy(lbufs[b].at[pl.ds(0, rows), :], l_hbm.at[pl.ds(pl.multiple_of(row0, 16), rows), cols(k, tok)], lsem.at[b])

    def tile(row0, rows, k, b, masked):
        group = min(4, rows // 8)
        sub_rows = lax.broadcasted_iota(jnp.int32, (8, lane), 0)
        for c0 in range(0, tok, sub):
            logits = dot_nt(w[pl.ds(pl.multiple_of(row0, 16), rows), :], z[pl.ds(pl.multiple_of(k * tok + c0, sub), sub), :]) * LOG2E
            if masked:
                ids = lax.broadcasted_iota(jnp.int32, (rows, sub), 0)
                logits = jnp.where(ids < jnp.where(me == n - 1, sz.solid, sz.rem), logits, NEG)
            lbufs[b][0:rows, c0:c0 + sub] = logits
            for c1 in range(0, sub, lane):
                sl = pl.ds(pl.multiple_of(k * tok + c0 + c1, lane), lane)
                big, tot, got = m[:, sl], s[:, sl], hit[:, sl]
                rel = lab[0:1, sl] - row0 - sub_rows
                for g in range(0, rows // 8, group):
                    part = [logits[8 * r:8 * r + 8, c1:c1 + lane] for r in range(g, min(g + group, rows // 8))]
                    new = functools.reduce(jnp.maximum, part, big)
                    tot = tot * jnp.exp2(big - new)
                    for r, x in enumerate(part):
                        tot += jnp.exp2(x - new)
                        got += jnp.where(rel == 8 * (g + r), x, 0.0)
                    big = new
                m[:, sl], s[:, sl], hit[:, sl] = big, tot, got

    def chunk_rows(row0, rows, first, masked):
        def step(i, _):
            for b in (0, 1):
                k = 2 * i + b

                @pl.when(jnp.logical_not(jnp.logical_and(first, i == 0)))
                def _():
                    out_copy(0, chunk if not masked else rows, 0, b).wait()
                tile(row0, rows, k, b, masked)
                out_copy(row0, rows, k, b).start()
            return 0
        lax.fori_loop(0, n_tok // 2, step, 0)

    def full_chunk(c, _):
        local(c, c * chunk, chunk).wait()
        for k in range(1, n):
            arrival(k, c, c * chunk, chunk).wait_recv()

        @pl.when(c + ahead < sz.full)
        def _():
            issue(c + ahead)

        @pl.when(c + ahead == sz.full)
        def _():
            issue_rem()
        chunk_rows(c * chunk, chunk, c == 0, False)
        return 0

    lax.fori_loop(0, sz.full, full_chunk, 0)
    for b in (0, 1):
        out_copy(0, chunk, 0, b).wait()
    local(sz.full, row_rem, sz.solid).wait()
    when_not_last(me, lambda: local(sz.full + 1, row_odd, sz.short).wait())
    for k in range(1, n):
        arrival(k, sz.full, row_rem, sz.solid).wait_recv()
        when_not_last(me, lambda: arrival(k, sz.full + 1, row_odd, sz.short).wait_recv())
    w_out = pltpu.make_async_copy(w, wb_hbm, osem.at[1])
    w_out.start()
    chunk_rows(row_rem, sz.rem, True, True)
    for b in (0, 1):
        out_copy(0, sz.rem, 0, b).wait()

    big = jnp.max(m[...], axis=0, keepdims=True)
    st_loc[0:1, :] = big
    st_loc[1:2, :] = jnp.sum(s[...] * jnp.exp2(m[...] - big), axis=0, keepdims=True)
    st_loc[2:3, :] = jnp.sum(hit[...], axis=0, keepdims=True)
    st_loc[3:8, :] = jnp.zeros((5, tokens), f32)

    own = tokens // at.n_all

    def block(tp, f):
        return pl.ds(pl.multiple_of((f * at.n_tp + tp) * own, own), own)

    mine = block(at.tp, at.f)

    def ask(k):
        tp, f = at.other(k)
        return rcopy(st_loc.at[:, block(tp, f)], got.at[k], ssend.at[k], srecv.at[k], dev(tp, f))

    def answer(k):
        tp, f = at.other(k)
        return rcopy(res, st.at[:, mine], rsend.at[k], rrecv.at[k], dev(tp, f))

    def answered(k):
        tp, f = at.other(at.n_all - k)
        return rcopy(res, st.at[:, block(tp, f)], rsend.at[k], rrecv.at[k], dev(tp, f))

    def every(fn):
        def go(k, _):
            fn(k)
            return 0
        lax.fori_loop(1, at.n_all, go, 0)

    every(lambda k: ask(k).start())
    got[0] = st_loc[:, mine]
    every(lambda k: ask(k).wait_recv())
    tops = got[:, 0:1, :]
    top = jnp.max(tops, axis=0)
    lse = top + jnp.log2(jnp.sum(got[:, 1:2, :] * jnp.exp2(tops - top[None]), axis=0))
    sc = scale[0:1, mine]
    res[0:1, :] = lse - jnp.log2(sc)
    res[1:2, :] = sc
    res[2:3, :] = (lse - jnp.sum(got[:, 2:3, :], axis=0)) * (sc * (1.0 / LOG2E))
    res[3:8, :] = jnp.zeros((5, own), f32)
    every(lambda k: answer(k).start())
    st[:, mine] = res[...]
    every(lambda k: answered(k).wait_recv())
    st_out[...] = st[...]
    every(lambda k: ask(k).wait_send())
    every(lambda k: answer(k).wait_send())
    z_out.wait()
    w_out.wait()

    def drain(c, _):
        for k in range(1, n):
            remote(k, c, c * chunk, chunk).wait_send()
        return 0

    lax.fori_loop(0, sz.full, drain, 0)
    for k in range(1, n):
        remote(k, sz.full, row_rem, sz.solid).wait_send()
        when_not_last(lax.rem(me + k, n), lambda: remote(k, sz.full + 1, row_odd, sz.short).wait_send())


def grad_kernel(sz, n_tp, chunk, early, tok, tok_own, half, z_hbm, w_hbm, l_hbm, st, lab, hid, gain, g_hbm, dw_hbm, gh_hbm, gg_out,
                z, w, l0, l1, g0, g1, q0, q1, acc, stage, acc_own, stage_own, sib_out, sib_in, pair_sum, y_out, y_in, part, z_out, z_in, z_own, x_out, x_in, gh, gg, gg_in,
                zsem, wsem, lsem, gsem, qsem, bsem, ssem, dw_send, dw_recv, own_sem, sib_s, sib_r, y_s, y_r, zz_s, zz_r, x_s, x_r, ag_s, ag_r, fw_s, fw_r, gh_sem, gain_s, gain_r):
    at = Place(sz.n, n_tp)
    me, n = at.f, sz.n
    tokens, width = z.shape[0], dw_hbm.shape[1]
    per_f, per_tp = tokens // n, tokens // at.n_all
    n_z, groups = at.n_z, 2 * at.n_z
    rounds = per_tp // half
    lbufs, gbufs, qbufs = (l0, l1), (g0, g1), (q0, q1)
    lane = min(128, tok)
    row_rem, row_low = sz.full * chunk, early * chunk
    low = [(j, chunk) for j in range(sz.full - early)] + [(sz.full - early, sz.rem)]
    far, sib = 1 - at.x, at.x * 2 + 1 - at.c
    sibling, y_peer, x_peer = dev(at.tp, sib), dev(at.z * 2 + 1 - at.y, at.f), dev(at.tp, far * 2 + at.c)

    z_load = pltpu.make_async_copy(z_hbm, z, zsem.at[0])
    w_load = pltpu.make_async_copy(w_hbm, w, wsem.at[0])
    z_load.start()
    w_load.start()

    def rows_at(row0, rows):
        return pl.ds(pl.multiple_of(row0, 16), rows)

    def gradient(x, top, sc, rel):
        rows = x.shape[0]
        p = jnp.exp2(x - top).reshape(rows // 8, 8, x.shape[1])
        ids = lax.broadcasted_iota(jnp.int32, p.shape, 0) * 8
        return jnp.where(ids == rel[None], p - sc[None], p).reshape(x.shape).astype(bf16)

    def token_row(sl, row0):
        size = sl.size
        return st[0:1, sl], st[1:2, sl], lab[0:1, sl] - row0 - lax.broadcasted_iota(jnp.int32, (8, size), 0)

    def load_l(row0, rows, k, b):
        return pltpu.make_async_copy(l_hbm.at[rows_at(row0, rows), cols(k, tok)], lbufs[b].at[pl.ds(0, rows), :], lsem.at[b])

    def load_g(row0, rows, k, b):
        return pltpu.make_async_copy(g_hbm.at[rows_at(row0, rows), cols(k, tok)], gbufs[b].at[pl.ds(0, rows), :], gsem.at[b])

    def save_g(row0, rows, k, b):
        return pltpu.make_async_copy(gbufs[b].at[pl.ds(0, rows), :], g_hbm.at[rows_at(row0, rows), cols(k, tok)], gsem.at[b])

    n_tok = tokens // tok
    step = min(256, tok)
    n_far = 2 * width

    def tile(row0, rows, k, b, fresh):
        total = None
        for c0 in range(0, tok, step):
            if fresh:
                for c1 in range(c0, c0 + step, lane):
                    top, sc, rel = token_row(pl.ds(pl.multiple_of(k * tok + c1, lane), lane), row0)
                    gbufs[b][0:rows, c1:c1 + lane] = gradient(lbufs[b][0:rows, c1:c1 + lane], top, sc, rel)
            lhs = gbufs[b][0:rows, c0:c0 + step]
            rhs = pl.ds(pl.multiple_of(k * tok + c0, step), step)
            d = (dot_nn(lhs, z[rhs, cols(far, n_far)]), dot_nn(lhs, z[rhs, cols(sib, width)]))
            total = d if total is None else (total[0] + d[0], total[1] + d[1])
        acc[0:rows, 0:n_far] += total[0]
        acc[0:rows, n_far:] += total[1]

    def sends(slot, row0, rows):
        out = []
        for i, f in enumerate((far * 2, far * 2 + 1, sib)):
            k = lax.rem(f + n - me, n)
            out.append(rcopy(stage.at[slot, pl.ds(0, rows), i * width:(i + 1) * width], dw_hbm.at[rows_at(me * sz.rows + row0, rows), :],
                             dw_send.at[slot, i], dw_recv.at[k], dev(at.tp, f)))
        return out

    def ship(c, row0, rows):
        slot = lax.rem(c, 2)

        @pl.when(c >= 2)
        def _():
            for cp in sends(slot, 0, chunk):
                cp.wait_send()
        stage[slot, 0:rows, :] = acc[0:rows, :].astype(bf16)
        acc[...] = jnp.zeros(acc.shape, f32)
        for cp in sends(slot, row0, rows):
            cp.start()

    enter(at)
    acc[...] = jnp.zeros(acc.shape, f32)
    for b in (0, 1):
        load_l(0, chunk, b, b).start()
    z_load.wait()

    def early_chunk(c, _):
        def pair(i, _):
            for b in (0, 1):
                k = 2 * i + b
                load_l(0, chunk, 0, b).wait()

                @pl.when(jnp.logical_not(jnp.logical_and(c == 0, i == 0)))
                def _():
                    save_g(0, chunk, 0, b).wait()
                tile(c * chunk, chunk, k, b, True)
                save_g(c * chunk, chunk, k, b).start()
                wrap = k + 2 >= n_tok
                c2 = jnp.where(wrap, c + 1, c)

                @pl.when(c2 < early)
                def _():
                    load_l(c2 * chunk, chunk, jnp.where(wrap, k + 2 - n_tok, k + 2), b).start()
            return 0
        lax.fori_loop(0, n_tok // 2, pair, 0)
        ship(c, c * chunk, chunk)
        return 0

    lax.fori_loop(0, early, early_chunk, 0)
    for b in (0, 1):
        save_g(0, chunk, 0, b).wait()
    w_load.wait()

    def group_of(q):
        r, g = q // groups, lax.rem(q, groups)
        xi, jj = g // n_z, lax.rem(g, n_z)
        return r, xi, jj, jnp.where(xi == 0, far, at.x), lax.rem(at.z + jj + 1, n_z)

    def pieces(q, own):
        r, _, _, xb, zb = group_of(q)
        cb = at.c if own else 1 - at.c
        return [pl.multiple_of((xb * 2 + cb) * per_f + (zb * 2 + yb) * per_tp + r * half, half) for yb in (1 - at.y, at.y)]

    def block_loads(q, b):
        out = []
        for i, t0 in enumerate(pieces(q, b == 1)):
            dst = pl.ds(i * half, half)
            out.append(pltpu.make_async_copy(g_hbm.at[pl.ds(0, row_low), pl.ds(t0, half)], qbufs[b].at[pl.ds(0, row_low), dst], qsem.at[b, i]))
            for j, rows in low:
                out.append(pltpu.make_async_copy(l_hbm.at[pl.ds(row_low + j * chunk, rows), pl.ds(t0, half)],
                                                 lbufs[b].at[pl.ds(0, rows), pl.ds((2 * j + i) * half, half)], bsem.at[b, 2 * j + i]))
        return out

    def block_saves(q, b):
        return [pltpu.make_async_copy(qbufs[b].at[pl.ds(row_low, sz.rows - row_low), pl.ds(i * half, half)],
                                      g_hbm.at[pl.ds(row_low, sz.rows - row_low), pl.ds(t0, half)], ssem.at[b, i]) for i, t0 in enumerate(pieces(q, b == 1))]

    def block_dot(q, b):
        for i, t0 in enumerate(pieces(q, b == 1)):
            for j, rows in low:
                row0 = row_low + j * chunk
                top, sc, rel = token_row(pl.ds(t0, half), row0)
                qbufs[b][row0:row0 + rows, i * half:(i + 1) * half] = gradient(lbufs[b][0:rows, (2 * j + i) * half:(2 * j + i + 1) * half], top, sc, rel)
        return dot_tn(qbufs[b][...], w[...])

    def to_sib(q):
        slot = lax.rem(q, 2)
        return rcopy(sib_out.at[slot], sib_in.at[slot], sib_s.at[slot], sib_r.at[slot], sibling)

    def to_y(q):
        slot, land = lax.rem(q, 2), lax.rem(q, y_in.shape[0])
        return rcopy(y_out.at[slot], y_in.at[land], y_s.at[slot], y_r.at[land], y_peer)

    def to_z(q):
        r, xi, jj, _, zb = group_of(q)
        return rcopy(z_out.at[jj], z_in.at[r, xi, jj], zz_s.at[jj], zz_r.at[r, xi, jj], dev(zb * 2 + at.y, at.f))

    def to_x(r):
        return rcopy(x_out, x_in.at[r], x_s.at[0], x_r.at[r], x_peer)

    def z_stage(q):
        _, xi, jj, _, _ = group_of(q)
        to_y(q).wait_recv()
        val = part[lax.rem(q, part.shape[0])] + y_in[lax.rem(q, y_in.shape[0])].astype(f32)

        @pl.when(jj == n_z - 1)
        def _():
            z_own[xi] = val

        @pl.when(jj < n_z - 1)
        def _():
            @pl.when(q >= n_z)
            def _():
                to_z(q - n_z).wait_send()
            z_out[jj] = val.astype(bf16)
            to_z(q).start()

    def z_sum(r, xi):
        val = z_own[xi]
        for jj in range(n_z - 1):
            rcopy(z_out.at[0], z_in.at[r, xi, jj], zz_s.at[jj], zz_r.at[r, xi, jj], sibling).wait_recv()
            val = val + z_in[r, xi, jj].astype(f32)
        return val

    def x_stage(r):
        @pl.when(r > 0)
        def _():
            to_x(0).wait_send()
        x_out[...] = z_sum(r, 0)
        to_x(r).start()

    def home(tp, r):
        return gh_hbm.at[pl.ds(pl.multiple_of(tp * per_tp + r * half, half), half), :]

    def gathers(r):
        out = [rcopy(gh.at[r], home(at.tp, r), ag_s.at[r, n_z - 1], fw_r.at[r, at.z], y_peer)]
        for jj in range(n_z - 1):
            to = lax.rem(at.z + jj + 1, n_z)
            out.append(rcopy(gh.at[r], home(at.tp, r), ag_s.at[r, jj], ag_r.at[r, jj], dev(to * 2 + at.y, at.f)))
        return out

    def keep(r):
        return pltpu.make_async_copy(gh.at[r], home(at.tp, r), gh_sem.at[r])

    def from_z(jj):
        return lax.rem(at.z + n_z - jj - 1, n_z)

    def arrived(r, jj):
        return rcopy(gh.at[r], home(from_z(jj) * 2 + at.y, r), ag_s.at[r, jj], ag_r.at[r, jj], sibling)

    def onward(r, jj):
        here = home(from_z(jj) * 2 + at.y, r)
        return rcopy(here, here, fw_s.at[r, jj], fw_r.at[r, from_z(jj)], y_peer)

    def final(r):
        to_x(r).wait_recv()
        dz = z_sum(r, 1) + x_in[r]
        h = hid[pl.ds(pl.multiple_of(r * half, half), half), :].astype(f32)
        inv = lax.rsqrt(jnp.mean(h * h, axis=-1, keepdims=True) + NORM_EPS)
        normed = h * inv
        a = dz * gain[...].astype(f32)
        gh[r] = (inv * (a - normed * jnp.mean(a * normed, axis=-1, keepdims=True))).astype(bf16)
        gg[...] += jnp.sum(dz * normed, axis=0, keepdims=True)
        keep(r).start()
        for cp in gathers(r):
            cp.start()

    def forwards(r):
        for jj in range(n_z - 1):
            arrived(r, jj).wait_recv()
            onward(r, jj).start()

    gg[...] = jnp.zeros(gg.shape, f32)
    last = rounds * groups
    x_at, final_at, forward_at = n_z + 2, groups + 2, groups + 6
    for b in (0, 1):
        for cp in block_loads(0, b):
            cp.start()

    def event(q, first, fn):
        @pl.when(jnp.logical_and(q >= first, jnp.logical_and(lax.rem(q + groups - first, groups) == 0, q < first + last)))
        def _():
            fn((q - first) // groups)

    def events(q):
        @pl.when(jnp.logical_and(q >= 2, q < last + 2))
        def _():
            z_stage(q - 2)
        event(q, x_at, x_stage)
        event(q, final_at, final)
        event(q, forward_at, forwards)

    def dz_group(q, _):
        for b in (0, 1):
            for cp in block_loads(q, b):
                cp.wait()

            @pl.when(q > 0)
            def _():
                for cp in block_saves(q - 1, b):
                    cp.wait()
            slot = lax.rem(q, 2)
            if b == 0:
                @pl.when(q >= 2)
                def _():
                    to_sib(q - 2).wait_send()
                sib_out[slot] = block_dot(q, b).astype(bf16)
                to_sib(q).start()
            else:
                @pl.when(q >= 2)
                def _():
                    to_y(q - 2).wait_send()
                pair_sum[...] = block_dot(q, b)
                to_sib(q).wait_recv()
                val = pair_sum[...] + sib_in[slot].astype(f32)
                y_out[slot] = val[0:half].astype(bf16)
                part[lax.rem(q, part.shape[0])] = val[half:]
                to_y(q).start()
            for cp in block_saves(q, b):
                cp.start()

            @pl.when(q + 1 < last)
            def _():
                for cp in block_loads(q + 1, b):
                    cp.start()
        events(q)
        return 0

    lax.fori_loop(0, last, dz_group, 0)
    for b in (0, 1):
        for cp in block_saves(last - 1, b):
            cp.wait()

    def stored(lo, tile_fn, after):
        for b in (0, 1):
            load_g(lo * chunk, chunk, b, b).start()

        def one(c, _):
            def pair(i, _):
                for b in (0, 1):
                    k = 2 * i + b
                    load_g(0, chunk, 0, b).wait()
                    tile_fn(c * chunk, chunk, k, b)
                    wrap = k + 2 >= n_tok
                    c2, k2 = jnp.where(wrap, c + 1, c), jnp.where(wrap, k + 2 - n_tok, k + 2)

                    @pl.when(c2 < sz.full)
                    def _():
                        load_g(c2 * chunk, chunk, k2, b).start()

                    @pl.when(c2 == sz.full)
                    def _():
                        load_g(row_rem, sz.rem, k2, b).start()
                return 0
            lax.fori_loop(0, n_tok // 2, pair, 0)
            after(c, c * chunk, chunk)
            return 0
        lax.fori_loop(lo, sz.full, one, 0)

        def pair(i, _):
            for b in (0, 1):
                k = 2 * i + b
                load_g(row_rem, sz.rem, 0, b).wait()
                tile_fn(row_rem, sz.rem, k, b)

                @pl.when(k + 2 < n_tok)
                def _():
                    load_g(row_rem, sz.rem, k + 2, b).start()
            return 0
        lax.fori_loop(0, n_tok // 2, pair, 0)
        after(sz.full, row_rem, sz.rem)

    def ship_and_sum(c, row0, rows):
        ship(c, row0, rows)
        if rows == chunk:
            e = last + 2 * (c - early)

            @pl.when(e < last + 4)
            def _():
                events(e)
                events(e + 1)

    stored(early, lambda row0, rows, k, b: tile(row0, rows, k, b, False), ship_and_sum)

    def tell_gain(k):
        tp, f = at.other(k)
        return rcopy(gg, gg_in.at[at.index], gain_s.at[k], gain_r.at[k], dev(tp, f))

    def heard_gain(k):
        i = lax.rem(at.index + at.n_all - k, at.n_all)
        return rcopy(gg, gg_in.at[i], gain_s.at[k], gain_r.at[k], sibling)

    def every(fn):
        def go(k, _):
            fn(k)
            return 0
        lax.fori_loop(1, at.n_all, go, 0)

    every(lambda k: tell_gain(k).start())
    gg_in[at.index] = gg[...]

    def tile_own(row0, rows, k, b):
        acc_own[0:rows, :] += dot_nn(gbufs[b][0:rows, :], z[cols(k, tok), cols(me, width)])

    def put_own(slot, row0, rows):
        return pltpu.make_async_copy(stage_own.at[slot, pl.ds(0, rows), :], dw_hbm.at[rows_at(me * sz.rows + row0, rows), :], own_sem.at[slot])

    def ship_own(c, row0, rows):
        slot = lax.rem(c, 2)

        @pl.when(c >= 2)
        def _():
            put_own(slot, 0, chunk).wait()
        stage_own[slot, 0:rows, :] = acc_own[0:rows, :].astype(bf16)
        acc_own[...] = jnp.zeros(acc_own.shape, f32)
        put_own(slot, row0, rows).start()
        if rows == chunk:
            @pl.when(c == min(6, sz.full - 1))
            def _():
                forwards(rounds - 1)

    acc_own[...] = jnp.zeros(acc_own.shape, f32)
    stored(0, tile_own, ship_own)

    every(lambda k: heard_gain(k).wait_recv())
    gg_out[...] = jnp.sum(gg_in[...], axis=0)
    every(lambda k: tell_gain(k).wait_send())
    put_own((sz.full - 1) % 2, 0, chunk).wait()
    put_own(sz.full % 2, 0, sz.rem).wait()
    for slot, rows in (((sz.full - 1) % 2, chunk), (sz.full % 2, sz.rem)):
        for cp in sends(slot, 0, rows):
            cp.wait_send()
    for q in (last - 2, last - 1):
        to_sib(q).wait_send()
        to_y(q).wait_send()
    for q in range(last - n_z, last - 1):
        to_z(q).wait_send()
    to_x(rounds - 1).wait_send()
    for r in range(rounds):
        keep(r).wait()
        for cp in gathers(r):
            cp.wait_send()
        for jj in range(n_z - 1):
            onward(r, jj).wait_send()
        for zf in range(n_z):
            rcopy(gh.at[r], home(zf * 2 + 1 - at.y, r), ag_s.at[r, 0], fw_r.at[r, zf], y_peer).wait_recv()
    for k in range(1, n):
        src = lax.rem(me + n - k, n)
        rcopy(dw_hbm.at[pl.ds(0, sz.rows), :], dw_hbm.at[rows_at(src * sz.rows, sz.rows), :], dw_send.at[0, 0], dw_recv.at[k], sibling).wait_recv()


HBM = pl.BlockSpec(memory_space=pl.ANY)
VM = pl.BlockSpec(memory_space=pltpu.VMEM)
DMA = pltpu.SemaphoreType.DMA


def params(**kw):
    return pltpu.CompilerParams(vmem_limit_bytes=VMEM_LIMIT, **kw)


def solution(mesh, chunk=CHUNK, tok=TOK, early=EARLY, z_rows=Z_ROWS):
    n_fsdp, n_tp = mesh.shape['fsdp'], mesh.shape['tp']
    n_all, n_z = n_fsdp * n_tp, n_tp // 2
    everyone = ('fsdp', 'tp')
    S = jax.ShapeDtypeStruct

    def per_device(hidden, labels, tok_mask, norm_gain, w_rows):
        fsdp_id, tp_id = lax.axis_index('fsdp'), lax.axis_index('tp')
        d = hidden.shape[1]
        width, vocab_tp = w_rows.shape
        tokens = hidden.shape[0] * n_fsdp
        sz = Sizes(vocab_tp, n_fsdp, chunk)
        own = hidden.shape[0] // n_tp
        half = own // 2
        rounds = 2
        hid_own = lax.dynamic_slice_in_dim(hidden, tp_id * own, own, 0)
        hid_all = lax.all_gather(hid_own, everyone, axis=0, tiled=True)
        lab_all = lax.all_gather(labels, 'fsdp', axis=0, tiled=True)
        mask_all = lax.all_gather(tok_mask, 'fsdp', axis=0, tiled=True)
        scale = (mask_all / jnp.sum(mask_all))[None, :]
        mine = lab_all // vocab_tp == tp_id
        lab_loc = jnp.where(mine, lab_all - tp_id * vocab_tp - fsdp_id * sz.rows, -1)[None, :]
        V = pltpu.VMEM

        logits, z_all, w_blk, st = pl.pallas_call(
            functools.partial(logits_kernel, sz, n_tp, chunk, tok),
            out_shape=(S((sz.rows, tokens), f32), S((tokens, d), bf16), S((sz.rows, d), bf16), S((8, tokens), f32)),
            in_specs=[HBM, HBM, VM, VM, VM], out_specs=(HBM, HBM, HBM, VM),
            scratch_shapes=[V((tokens, d), bf16), V((sz.rows, d), bf16), V((chunk, tok), f32), V((chunk, tok), f32),
                            V((z_rows, d), bf16), V((z_rows, d), bf16),
                            V((8, tokens), f32), V((8, tokens), f32), V((8, tokens), f32),
                            V((8, tokens), f32), V((n_all, 8, own), f32), V((8, own), f32), V((8, tokens), f32),
                            DMA((sz.full + 2, n_fsdp)), DMA((sz.full + 2, n_fsdp)), DMA((sz.full + 2,)), DMA((2,)), DMA((2,)), DMA((2,)),
                            DMA((n_all,)), DMA((n_all,)), DMA((n_all,)), DMA((n_all,))],
            compiler_params=params(collective_id=0, has_side_effects=True), name='logits',
        )(hid_all, w_rows.T, norm_gain[None, :], lab_loc, scale)

        mean_loss = jnp.sum(st[2])
        n_low = sz.full - early + 1

        _, dw_t, grad_hidden, gain_sum = pl.pallas_call(
            functools.partial(grad_kernel, sz, n_tp, chunk, early, tok, tok, half),
            out_shape=(S((sz.rows, tokens), bf16), S((n_fsdp * sz.rows, width), bf16), S(hidden.shape, bf16), S((1, d), f32)),
            in_specs=[HBM, HBM, HBM, VM, VM, VM, VM], out_specs=(HBM, HBM, HBM, VM),
            scratch_shapes=[V((tokens, d), bf16), V((sz.rows, d), bf16), V((chunk, tok), f32), V((chunk, tok), f32), V((chunk, tok), bf16), V((chunk, tok), bf16),
                            V((sz.rows, 2 * half), bf16), V((sz.rows, 2 * half), bf16),
                            V((chunk, 3 * width), f32), V((2, chunk, 3 * width), bf16), V((chunk, width), f32), V((2, chunk, width), bf16),
                            V((2, 2 * half, d), bf16), V((2, 2 * half, d), bf16), V((2 * half, d), f32), V((2, half, d), bf16), V((8, half, d), bf16), V((3, half, d), f32),
                            V((n_z - 1, half, d), bf16), V((rounds, 2, n_z - 1, half, d), bf16), V((2, half, d), f32), V((half, d), f32), V((rounds, half, d), f32),
                            V((rounds, half, d), bf16), V((1, d), f32), V((n_all, 1, d), f32),
                            DMA((1,)), DMA((1,)), DMA((2,)), DMA((2,)), DMA((2, 2)), DMA((2, 2 * n_low)), DMA((2, 2)),
                            DMA((2, 3)), DMA((n_fsdp,)), DMA((2,)), DMA((2,)), DMA((2,)), DMA((2,)), DMA((8,)),
                            DMA((n_z - 1,)), DMA((rounds, 2, n_z - 1)), DMA((1,)), DMA((rounds,)),
                            DMA((rounds, n_z)), DMA((rounds, n_z)), DMA((rounds, n_z)), DMA((rounds, n_z)), DMA((rounds,)), DMA((n_all,)), DMA((n_all,))],
            compiler_params=params(collective_id=1, has_side_effects=True), name='grads',
        )(z_all, w_blk, logits, st, lab_loc, hid_own, norm_gain[None, :])
        return mean_loss, grad_hidden, dw_t[:vocab_tp].T, gain_sum[0]

    return jax.shard_map(per_device, mesh=mesh, in_specs=(P('fsdp', None), P('fsdp'), P('fsdp'), P(), P('fsdp', 'tp')), out_specs=(P(), P('fsdp', None), P('fsdp', 'tp'), P()), check_vma=False)
```

time: 959 us -> 597 us (0.62)
  waiting for transfers between devices: 458 us -> 104 us
  Pallas kernels: 348 us -> 443 us
  blocking collectives: 93.9 us -> 11.6 us
    reduce_scatter x2 -> x0, waiting for transfers between devices: 201 us -> none  [the longest x1 123 us: per_device(): lax.psum_scatter(grad_part, 'fsdp', scatter_dimension=0, tiled=True)]
    psum x1 -> x0, waiting for transfers between devices: 122 us -> none  [per_device(): lax.psum(jnp.stack([stats[1] * jnp.exp2(stats[0] - big), stats[2]]), ever...]
    pallas_call x3 -> x2, Pallas kernels: 348 us -> 443 us  [the longest x1 299 us: per_device(): pl.pallas_call(functools.partial(grad_kernel, sz, n_tp, chunk, early, tok...]
    pmax x1 -> x0, blocking collectives: 41.1 us -> none  [per_device(): big = lax.pmax(stats[0], everyone)]
    psum x1 -> x0, blocking collectives: 41 us -> none  [per_device(): grad_gain = lax.psum(jnp.sum(grad_z * normed, axis=0), everyone)]
    all_to_all x1 -> x0, waiting for transfers between devices: 24.4 us -> none  [per_device(): lax.all_to_all(dw_t, 'fsdp', split_axis=1, concat_axis=0, tiled=True)]
  transfers between devices with their start and end apart: 6 -> 1, of which waited for: 5 -> 1; matrix products, arithmetic and copies ran while one was open for 2% -> 1% of each run, Pallas kernels for 0% -> 0%
where the time goes in v2:
time: 597 us; the launch traced here: 593 us
  Pallas kernels  443 us (74%)
  waiting for transfers between devices  104 us (17%)
  local copies, waits for them, and re-layouts  15.8 us (3%)
  between operations  14.1 us (2%)
  blocking collectives  11.6 us (2%)
    pallas_call x1, Pallas kernels, per_device(): pl.pallas_call(functools.partial(grad_kernel, sz, n_tp, chunk, early, tok...  299 us
    pallas_call x1, Pallas kernels, per_device(): pl.pallas_call(functools.partial(logits_kernel, sz, n_tp, chunk, tok), ou...  143 us
    all_gather x1, waiting for transfers between devices, per_device(): hid_all = lax.all_gather(hid_own, everyone, axis=0, tiled=True)  104 us
  transfers between devices with their start and end apart: 1, of which 1 were waited for; matrix products, arithmetic and copies ran while one was open for 1% of the time, Pallas kernels for 0%

profile of v2, /device:TPU:0, one launch (start us, length us, event | category | flops | bytes accessed | tf_op | source)
XLA Modules:
  0.0 592.6 jit_solution(8800981362039924629)
XLA Ops:
  7.2 0.0 all-gather.2.cloned.1.call-start
  7.2 1.9 constant_dynamic-slice_fusion.hid
  9.1 0.0 all-gather.2.cloned.1.call-update
  9.1 1.3 broadcast_in_dim.12.gain
  10.4 6.2 %all_gather.11 = f32[8192]{0:T(1024)S(1)} all-gather(f32[2048]{0:T(1024)} %param.7), channel_id=1, replica_groups=mesh['tp'=8,'fsdp'=4] {'fsdp'}, dimensions={0}, use_global_device_ids=true | all-gather | bytes 40960 | tf_op jit(solution)/shard_map/all_gather | solution.py:742
  16.6 0.6 reduce_sum.18
  17.2 5.4 all_gather.10
  22.6 1.3 broadcast_divide_fusion
  23.9 0.6 subtract_select_fusion
  24.5 104.1 %all-gather.2.cloned.1.call-done.h_hbm = bf16[8192,1024]{1,0:T(8,128)(2,1)} async-done(((bf16[256,1024]{1,0:T(8,128)(2,1)}), bf16[8192,1024]{1,0:T(8,128)(2,1)}) %all-gather.2.cloned.1.call-update) | async-done | bytes 16777232 | tf_op jit(solution)/shard_map/all_gather | solution.py:740
  128.6 143.4 %logits.1 = (f32[4752,8192]{1,0:T(8,128)}, bf16[8192,1024]{1,0:T(8,128)(2,1)}, bf16[4752,1024]{1,0:T(8,128)(2,1)}, f32[8,8192]{1,0:T(8,128)}) custom-call(bf16[8192,1024]{1,0:T(8,128)(2,1)} %all-gather.2.cloned.1.call-done.h_hbm, bf16[18992,256]{1,0:T(8,128)(2,1)} %bitcast.6, bf16[1,1024]{1,0:T(2,128)(2,1)} %broadcast_in_dim.12.gain, s32[1,8192]{1,0:T(1,128)} %bitcast.7, ...), custom_call_target="tpu_custom_call" | custom-call | tf_op jit(solution)/shard_map/logits/pallas_call | solution.py:748
  272.0 1.6 slice_reduce_fusion
  273.6 299.4 %grads.1 = (bf16[4752,8192]{1,0:T(8,128)(2,1)}, bf16[19008,256]{1,0:T(8,128)(2,1)}, bf16[2048,1024]{1,0:T(8,128)(2,1)}, f32[1,1024]{1,0:T(1,128)}) custom-call(bf16[8192,1024]{1,0:T(8,128)(2,1)} %get-tuple-element.12.z_hbm, bf16[4752,1024]{1,0:T(8,128)(2,1)} %get-tuple-element.13.w_hbm, f32[4752,8192]{1,0:T(8,128)} %get-tuple-element.14.l_hbm, ...), custom_call_target="tpu_custom_call" | custom-call | tf_op jit(solution)/shard_map/grads/pallas_call | solution.py:764
  573.1 0.0 copy-start
  573.1 0.0 copy-start.1
  573.1 10.0 %slice_bitcast_fusion = bf16[256,18992]{0,1:T(8,128)(2,1)} fusion(bf16[19008,256]{1,0:T(8,128)(2,1)} %get-tuple-element.16), kind=kLoop, calls=%fused_computation | loop fusion | bytes 19447808 | tf_op jit(solution)/shard_map/transpose | solution.py:780
  583.1 0.0 copy-done
  583.1 2.0 copy.11
  585.1 0.0 copy-done.1
  585.1 0.6 copy.12
Async XLA Ops:
  7.2 121.4 %all-gather.2.cloned.1.call-start = ((), (), s32[]{:S(2)}) async-start(), calls=%async_computation | async-start | bytes 17301504 | tf_op jit(solution)/shard_map/all_gather | solution.py:740
  573.1 10.0 %copy-start = (bf16[2048,1024]{1,0:T(8,128)(2,1)S(1)}, bf16[2048,1024]{1,0:T(8,128)(2,1)}, u32[]{:S(2)}) copy-start(bf16[2048,1024]{1,0:T(8,128)(2,1)} %get-tuple-element.23) | copy-start | bytes 12582916
  573.1 12.1 %copy-start.1 = (f32[1,1024]{1,0:T(1,128)S(1)}, f32[1,1024]{1,0:T(1,128)}, u32[]{:S(2)}) copy-start(f32[1,1024]{1,0:T(1,128)} %get-tuple-element.17) | copy-start | bytes 12292
Sparse Core Ops, SparseCore 0:
  11.6 116.8 all-gather.1

commit v3 on v2

--- a/solution.py
+++ b/solution.py
@@ -12,11 +12,12 @@
 NEG = -1e30
 CHUNK = 512
 TOK = 2048
-EARLY = 6
+EARLY = 4
 Z_ROWS = 512
 AHEAD = 5
 VMEM_LIMIT = 67_043_328
 MESH = pl.DeviceIdType.MESH
+scope = jax.named_scope
 f32, bf16 = jnp.float32, jnp.bfloat16
 
 
@@ -81,14 +82,15 @@
     pl.semaphore_wait(barrier, at.n_all - 1)
 
 
-def logits_kernel(sz, n_tp, chunk, tok, h_hbm, w_hbm, gain, lab, scale, l_hbm, z_hbm, wb_hbm, st_out, z, w, lb0, lb1, hb0, hb1, m, s, hit, st_loc, got, res, st, send, recv, loc, hsem, lsem, osem, ssend, srecv, rsend, rrecv):
+def logits_kernel(sz, n_tp, chunk, tok, h_hbm, w_hbm, gain, lab, scale, l_hbm, z_hbm, wb_hbm, st_out, hit_out, z, w, lb0, lb1, hb0, hb1, m, s, hit, st_loc, got, res, st, send, recv, loc, hsem, lsem, osem, ssend, srecv, rsend, rrecv):
     at = Place(sz.n, n_tp)
     me = at.f
     n, width = sz.n, w_hbm.shape[1]
     tokens = h_hbm.shape[0]
     lbufs, hbufs = (lb0, lb1), (hb0, hb1)
 
-    enter(at)
+    with scope('enter'):
+        enter(at)
 
     def remote(k, c, row0, rows):
         dest = lax.rem(me + k, n)
@@ -159,7 +161,8 @@
                 load_h(k + 2, b).start()
         return 0
 
-    lax.fori_loop(0, n_z // 2, norm, 0)
+    with scope('norm'):
+        lax.fori_loop(0, n_z // 2, norm, 0)
     z_out = pltpu.make_async_copy(z, z_hbm, osem.at[0])
     z_out.start()
 
@@ -201,18 +204,21 @@
             for b in (0, 1):
                 k = 2 * i + b
 
-                @pl.when(jnp.logical_not(jnp.logical_and(first, i == 0)))
-                def _():
-                    out_copy(0, chunk if not masked else rows, 0, b).wait()
-                tile(row0, rows, k, b, masked)
+                with scope('l_wait'):
+                    @pl.when(jnp.logical_not(jnp.logical_and(first, i == 0)))
+                    def _():
+                        out_copy(0, chunk if not masked else rows, 0, b).wait()
+                with scope('l_tile'):
+                    tile(row0, rows, k, b, masked)
                 out_copy(row0, rows, k, b).start()
             return 0
         lax.fori_loop(0, n_tok // 2, step, 0)
 
     def full_chunk(c, _):
-        local(c, c * chunk, chunk).wait()
-        for k in range(1, n):
-            arrival(k, c, c * chunk, chunk).wait_recv()
+        with scope('w_wait'):
+            local(c, c * chunk, chunk).wait()
+            for k in range(1, n):
+                arrival(k, c, c * chunk, chunk).wait_recv()
 
         @pl.when(c + ahead < sz.full)
         def _():
@@ -241,8 +247,6 @@
     big = jnp.max(m[...], axis=0, keepdims=True)
     st_loc[0:1, :] = big
     st_loc[1:2, :] = jnp.sum(s[...] * jnp.exp2(m[...] - big), axis=0, keepdims=True)
-    st_loc[2:3, :] = jnp.sum(hit[...], axis=0, keepdims=True)
-    st_loc[3:8, :] = jnp.zeros((5, tokens), f32)
 
     own = tokens // at.n_all
 
@@ -271,19 +275,23 @@
 
     every(lambda k: ask(k).start())
     got[0] = st_loc[:, mine]
-    every(lambda k: ask(k).wait_recv())
+    with scope('ask_wait'):
+        every(lambda k: ask(k).wait_recv())
     tops = got[:, 0:1, :]
     top = jnp.max(tops, axis=0)
-    lse = top + jnp.log2(jnp.sum(got[:, 1:2, :] * jnp.exp2(tops - top[None]), axis=0))
-    sc = scale[0:1, mine]
-    res[0:1, :] = lse - jnp.log2(sc)
-    res[1:2, :] = sc
-    res[2:3, :] = (lse - jnp.sum(got[:, 2:3, :], axis=0)) * (sc * (1.0 / LOG2E))
-    res[3:8, :] = jnp.zeros((5, own), f32)
+    res[...] = top + jnp.log2(jnp.sum(got[:, 1:2, :] * jnp.exp2(tops - top[None]), axis=0))
     every(lambda k: answer(k).start())
     st[:, mine] = res[...]
-    every(lambda k: answered(k).wait_recv())
-    st_out[...] = st[...]
+    loss_part = jnp.sum(hit[...] * scale[...], axis=0, keepdims=True)
+    hit_out[...] = jnp.broadcast_to(jnp.sum(loss_part, axis=1, keepdims=True), hit_out.shape)
+    with scope('answer_wait'):
+        every(lambda k: answered(k).wait_recv())
+    st_out[0:1, :] = st[...] - jnp.log2(scale[...])
+    st_out[1:2, :] = scale[...]
+    st_out[2:3, :] = st[...]
+    st_out[3:8, :] = jnp.zeros((5, tokens), f32)
+    scope_tail = scope('l_tail')
+    scope_tail.__enter__()
     every(lambda k: ask(k).wait_send())
     every(lambda k: answer(k).wait_send())
     z_out.wait()
@@ -298,11 +306,12 @@
     for k in range(1, n):
         remote(k, sz.full, row_rem, sz.solid).wait_send()
         when_not_last(lax.rem(me + k, n), lambda: remote(k, sz.full + 1, row_odd, sz.short).wait_send())
-
-
-def grad_kernel(sz, n_tp, chunk, early, tok, tok_own, half, z_hbm, w_hbm, l_hbm, st, lab, hid, gain, g_hbm, dw_hbm, gh_hbm, gg_out,
+    scope_tail.__exit__(None, None, None)
+
+
+def grad_kernel(sz, n_tp, chunk, early, tok, tok_own, half, z_hbm, w_hbm, l_hbm, st, lab, hid, gain, hit_sum, g_hbm, dw_hbm, gh_hbm, gg_out, ds_hbm,
                 z, w, l0, l1, g0, g1, q0, q1, acc, stage, acc_own, stage_own, sib_out, sib_in, pair_sum, y_out, y_in, part, z_out, z_in, z_own, x_out, x_in, gh, gg, gg_in,
-                zsem, wsem, lsem, gsem, qsem, bsem, ssem, dw_send, dw_recv, own_sem, sib_s, sib_r, y_s, y_r, zz_s, zz_r, x_s, x_r, ag_s, ag_r, fw_s, fw_r, gh_sem, gain_s, gain_r):
+                zsem, wsem, lsem, gsem, qsem, bsem, ssem, dw_copy, dw_send, dw_recv, own_sem, sib_s, sib_r, y_s, y_r, zz_s, zz_r, x_s, x_r, ag_s, ag_r, fw_s, fw_r, gh_sem, gain_s, gain_r):
     at = Place(sz.n, n_tp)
     me, n = at.f, sz.n
     tokens, width = z.shape[0], dw_hbm.shape[1]
@@ -316,9 +325,12 @@
     far, sib = 1 - at.x, at.x * 2 + 1 - at.c
     sibling, y_peer, x_peer = dev(at.tp, sib), dev(at.z * 2 + 1 - at.y, at.f), dev(at.tp, far * 2 + at.c)
 
-    z_load = pltpu.make_async_copy(z_hbm, z, zsem.at[0])
+    n_far = 2 * width
+    z_loads = [pltpu.make_async_copy(z_hbm.at[:, src], z.at[:, dst], zsem.at[i]) for i, (src, dst) in enumerate((
+        (cols(far, n_far), pl.ds(0, n_far)), (cols(sib, width), pl.ds(n_far, width)), (cols(me, width), pl.ds(n_far + width, width))))]
     w_load = pltpu.make_async_copy(w_hbm, w, wsem.at[0])
-    z_load.start()
+    for cp in z_loads:
+        cp.start()
     w_load.start()
 
     def rows_at(row0, rows):
@@ -345,58 +357,64 @@
 
     n_tok = tokens // tok
     step = min(256, tok)
-    n_far = 2 * width
 
     def tile(row0, rows, k, b, fresh):
+        mid = rows // 32 * 16
+        parts = ((0, rows, 0, n_far), (0, mid, n_far, n_far + width), (mid, rows, n_far, n_far + width))
         total = None
         for c0 in range(0, tok, step):
             if fresh:
                 for c1 in range(c0, c0 + step, lane):
                     top, sc, rel = token_row(pl.ds(pl.multiple_of(k * tok + c1, lane), lane), row0)
                     gbufs[b][0:rows, c1:c1 + lane] = gradient(lbufs[b][0:rows, c1:c1 + lane], top, sc, rel)
-            lhs = gbufs[b][0:rows, c0:c0 + step]
             rhs = pl.ds(pl.multiple_of(k * tok + c0, step), step)
-            d = (dot_nn(lhs, z[rhs, cols(far, n_far)]), dot_nn(lhs, z[rhs, cols(sib, width)]))
-            total = d if total is None else (total[0] + d[0], total[1] + d[1])
-        acc[0:rows, 0:n_far] += total[0]
-        acc[0:rows, n_far:] += total[1]
-
-    def sends(slot, row0, rows):
+            d = [dot_nn(gbufs[b][r0:r1, c0:c0 + step], z[rhs, v0:v1]) for r0, r1, v0, v1 in parts]
+            total = d if total is None else [p + q for p, q in zip(total, d)]
+        for (r0, r1, v0, v1), val in zip(parts, total):
+            acc[r0:r1, v0:v1] += val
+
+    def aside(c, rows):
+        slot = lax.rem(c, 2)
+        return pltpu.make_async_copy(stage.at[slot, pl.ds(0, rows), :], ds_hbm.at[rows_at(c * chunk, rows), :], dw_copy.at[slot])
+
+    def sends(c, rows):
         out = []
         for i, f in enumerate((far * 2, far * 2 + 1, sib)):
-            k = lax.rem(f + n - me, n)
-            out.append(rcopy(stage.at[slot, pl.ds(0, rows), i * width:(i + 1) * width], dw_hbm.at[rows_at(me * sz.rows + row0, rows), :],
-                             dw_send.at[slot, i], dw_recv.at[k], dev(at.tp, f)))
+            out.append(rcopy(ds_hbm.at[rows_at(c * chunk, rows), i * width:(i + 1) * width], dw_hbm.at[rows_at(me * sz.rows + c * chunk, rows), :],
+                             dw_send.at[c, i], dw_recv.at[lax.rem(f + n - me, n)], dev(at.tp, f)))
         return out
 
-    def ship(c, row0, rows):
-        slot = lax.rem(c, 2)
-
-        @pl.when(c >= 2)
-        def _():
-            for cp in sends(slot, 0, chunk):
-                cp.wait_send()
-        stage[slot, 0:rows, :] = acc[0:rows, :].astype(bf16)
+    def ship(c, rows):
+        stage[lax.rem(c, 2), 0:rows, :] = acc[0:rows, :].astype(bf16)
         acc[...] = jnp.zeros(acc.shape, f32)
-        for cp in sends(slot, row0, rows):
+        aside(c, rows).start()
+
+    def flush(c, rows):
+        aside(c, rows).wait()
+        for cp in sends(c, rows):
             cp.start()
 
-    enter(at)
+    with scope('enter'):
+        enter(at)
     acc[...] = jnp.zeros(acc.shape, f32)
     for b in (0, 1):
         load_l(0, chunk, b, b).start()
-    z_load.wait()
+    with scope('zload'):
+        for cp in z_loads:
+            cp.wait()
 
     def early_chunk(c, _):
         def pair(i, _):
             for b in (0, 1):
                 k = 2 * i + b
-                load_l(0, chunk, 0, b).wait()
-
-                @pl.when(jnp.logical_not(jnp.logical_and(c == 0, i == 0)))
-                def _():
-                    save_g(0, chunk, 0, b).wait()
-                tile(c * chunk, chunk, k, b, True)
+                with scope('b1_wait'):
+                    load_l(0, chunk, 0, b).wait()
+
+                    @pl.when(jnp.logical_not(jnp.logical_and(c == 0, i == 0)))
+                    def _():
+                        save_g(0, chunk, 0, b).wait()
+                with scope('b1_tile'):
+                    tile(c * chunk, chunk, k, b, True)
                 save_g(c * chunk, chunk, k, b).start()
                 wrap = k + 2 >= n_tok
                 c2 = jnp.where(wrap, c + 1, c)
@@ -404,9 +422,14 @@
                 @pl.when(c2 < early)
                 def _():
                     load_l(c2 * chunk, chunk, jnp.where(wrap, k + 2 - n_tok, k + 2), b).start()
+
+            @pl.when(jnp.logical_and(i == 0, c > 0))
+            def _():
+                flush(c - 1, chunk)
             return 0
         lax.fori_loop(0, n_tok // 2, pair, 0)
-        ship(c, c * chunk, chunk)
+        with scope('ship'):
+            ship(c, chunk)
         return 0
 
     lax.fori_loop(0, early, early_chunk, 0)
@@ -463,7 +486,8 @@
 
     def z_stage(q):
         _, xi, jj, _, _ = group_of(q)
-        to_y(q).wait_recv()
+        with scope('y_wait'):
+            to_y(q).wait_recv()
         val = part[lax.rem(q, part.shape[0])] + y_in[lax.rem(q, y_in.shape[0])].astype(f32)
 
         @pl.when(jj == n_z - 1)
@@ -489,7 +513,8 @@
         @pl.when(r > 0)
         def _():
             to_x(0).wait_send()
-        x_out[...] = z_sum(r, 0)
+        with scope('x_stage'):
+            x_out[...] = z_sum(r, 0).astype(bf16)
         to_x(r).start()
 
     def home(tp, r):
@@ -516,65 +541,60 @@
         return rcopy(here, here, fw_s.at[r, jj], fw_r.at[r, from_z(jj)], y_peer)
 
     def final(r):
-        to_x(r).wait_recv()
-        dz = z_sum(r, 1) + x_in[r]
+        with scope('final_wait'):
+            to_x(r).wait_recv()
+            dz = z_sum(r, 1) + x_in[r].astype(f32)
         h = hid[pl.ds(pl.multiple_of(r * half, half), half), :].astype(f32)
         inv = lax.rsqrt(jnp.mean(h * h, axis=-1, keepdims=True) + NORM_EPS)
         normed = h * inv
         a = dz * gain[...].astype(f32)
         gh[r] = (inv * (a - normed * jnp.mean(a * normed, axis=-1, keepdims=True))).astype(bf16)
-        gg[...] += jnp.sum(dz * normed, axis=0, keepdims=True)
+        gg[0:1, 0:gain.shape[1]] += jnp.sum(dz * normed, axis=0, keepdims=True)
         keep(r).start()
+
+    def gather_start(r):
         for cp in gathers(r):
             cp.start()
 
     def forwards(r):
         for jj in range(n_z - 1):
-            arrived(r, jj).wait_recv()
+            with scope('fw_wait'):
+                arrived(r, jj).wait_recv()
             onward(r, jj).start()
 
     gg[...] = jnp.zeros(gg.shape, f32)
+    gg[0:1, gain.shape[1]:] = hit_sum[...]
     last = rounds * groups
-    x_at, final_at, forward_at = n_z + 2, groups + 2, groups + 6
     for b in (0, 1):
         for cp in block_loads(0, b):
             cp.start()
 
-    def event(q, first, fn):
-        @pl.when(jnp.logical_and(q >= first, jnp.logical_and(lax.rem(q + groups - first, groups) == 0, q < first + last)))
-        def _():
-            fn((q - first) // groups)
-
-    def events(q):
-        @pl.when(jnp.logical_and(q >= 2, q < last + 2))
-        def _():
-            z_stage(q - 2)
-        event(q, x_at, x_stage)
-        event(q, final_at, final)
-        event(q, forward_at, forwards)
-
     def dz_group(q, _):
         for b in (0, 1):
-            for cp in block_loads(q, b):
-                cp.wait()
-
-            @pl.when(q > 0)
-            def _():
-                for cp in block_saves(q - 1, b):
+            with scope('a_wait'):
+                for cp in block_loads(q, b):
                     cp.wait()
+
+                @pl.when(q > 0)
+                def _():
+                    for cp in block_saves(q - 1, b):
+                        cp.wait()
             slot = lax.rem(q, 2)
             if b == 0:
                 @pl.when(q >= 2)
                 def _():
                     to_sib(q - 2).wait_send()
-                sib_out[slot] = block_dot(q, b).astype(bf16)
+                with scope('a_dot0'):
+                    sib_out[slot] = block_dot(q, b).astype(bf16)
                 to_sib(q).start()
             else:
                 @pl.when(q >= 2)
                 def _():
                     to_y(q - 2).wait_send()
-                pair_sum[...] = block_dot(q, b)
-                to_sib(q).wait_recv()
+                with scope('a_dot1'):
+                    pair_sum[...] = block_dot(q, b)
+                with scope('sib_wait'):
+                    to_sib(q).wait_recv()
                 val = pair_sum[...] + sib_in[slot].astype(f32)
                 y_out[slot] = val[0:half].astype(bf16)
                 part[lax.rem(q, part.shape[0])] = val[half:]
@@ -586,15 +606,32 @@
             def _():
                 for cp in block_loads(q + 1, b):
                     cp.start()
-        events(q)
+
+        @pl.when(q == 0)
+        def _():
+            flush(early - 1, chunk)
+
+        @pl.when(q >= 2)
+        def _():
+            z_stage(q - 2)
+
+        @pl.when(q == groups + 2)
+        def _():
+            x_stage(0)
+
+        @pl.when(q == last - 2)
+        def _():
+            final(0)
         return 0
 
     lax.fori_loop(0, last, dz_group, 0)
+    x_stage(1)
+    gather_start(0)
     for b in (0, 1):
         for cp in block_saves(last - 1, b):
             cp.wait()
 
-    def stored(lo, tile_fn, after):
+    def stored(lo, name, tile_fn, after, mid):
         for b in (0, 1):
             load_g(lo * chunk, chunk, b, b).start()
 
@@ -602,8 +639,10 @@
             def pair(i, _):
                 for b in (0, 1):
                     k = 2 * i + b
-                    load_g(0, chunk, 0, b).wait()
-                    tile_fn(c * chunk, chunk, k, b)
+                    with scope(name + '_wait'):
+                        load_g(0, chunk, 0, b).wait()
+                    with scope(name + '_tile'):
+                        tile_fn(c * chunk, chunk, k, b)
                     wrap = k + 2 >= n_tok
                     c2, k2 = jnp.where(wrap, c + 1, c), jnp.where(wrap, k + 2 - n_tok, k + 2)
 
@@ -614,9 +653,13 @@
                     @pl.when(c2 == sz.full)
                     def _():
                         load_g(row_rem, sz.rem, k2, b).start()
+
+                @pl.when(i == 0)
+                def _():
+                    mid(c)
                 return 0
             lax.fori_loop(0, n_tok // 2, pair, 0)
-            after(c, c * chunk, chunk)
+            after(c, chunk)
             return 0
         lax.fori_loop(lo, sz.full, one, 0)
 
@@ -629,21 +672,39 @@
                 @pl.when(k + 2 < n_tok)
                 def _():
                     load_g(row_rem, sz.rem, k + 2, b).start()
+
+            @pl.when(i == 0)
+            def _():
+                mid(sz.full)
             return 0
         lax.fori_loop(0, n_tok // 2, pair, 0)
-        after(sz.full, row_rem, sz.rem)
-
-    def ship_and_sum(c, row0, rows):
-        ship(c, row0, rows)
+        after(sz.full, sz.rem)
+
+    late = min(3, sz.full - early - 1)
+
+    def ship_and_sum(c, rows):
+        ship(c, rows)
         if rows == chunk:
-            e = last + 2 * (c - early)
-
-            @pl.when(e < last + 4)
+            @pl.when(c == early)
             def _():
-                events(e)
-                events(e + 1)
-
-    stored(early, lambda row0, rows, k, b: tile(row0, rows, k, b, False), ship_and_sum)
+                z_stage(last - 2)
+                z_stage(last - 1)
+
+            @pl.when(c == early + min(2, late))
+            def _():
+                final(1)
+                gather_start(1)
+
+            @pl.when(c == early + late)
+            def _():
+                forwards(0)
+
+    def flush_before(c):
+        @pl.when(c > early)
+        def _():
+            flush(c - 1, chunk)
+
+    stored(early, 'b2', lambda row0, rows, k, b: tile(row0, rows, k, b, False), ship_and_sum, flush_before)
 
     def tell_gain(k):
         tp, f = at.other(k)
@@ -663,12 +724,14 @@
     gg_in[at.index] = gg[...]
 
     def tile_own(row0, rows, k, b):
-        acc_own[0:rows, :] += dot_nn(gbufs[b][0:rows, :], z[cols(k, tok), cols(me, width)])
+        mid = rows // 32 * 16
+        for r0, r1 in ((0, mid), (mid, rows)):
+            acc_own[r0:r1, :] += dot_nn(gbufs[b][r0:r1, :], z[cols(k, tok), n_far + width:])
 
     def put_own(slot, row0, rows):
         return pltpu.make_async_copy(stage_own.at[slot, pl.ds(0, rows), :], dw_hbm.at[rows_at(me * sz.rows + row0, rows), :], own_sem.at[slot])
 
-    def ship_own(c, row0, rows):
+    def ship_own(c, rows):
         slot = lax.rem(c, 2)
 
         @pl.when(c >= 2)
@@ -676,22 +739,37 @@
             put_own(slot, 0, chunk).wait()
         stage_own[slot, 0:rows, :] = acc_own[0:rows, :].astype(bf16)
         acc_own[...] = jnp.zeros(acc_own.shape, f32)
-        put_own(slot, row0, rows).start()
+        put_own(slot, c * chunk, rows).start()
         if rows == chunk:
-            @pl.when(c == min(6, sz.full - 1))
+            @pl.when(c == min(5, sz.full - 1))
             def _():
                 forwards(rounds - 1)
 
     acc_own[...] = jnp.zeros(acc_own.shape, f32)
-    stored(0, tile_own, ship_own)
-
-    every(lambda k: heard_gain(k).wait_recv())
-    gg_out[...] = jnp.sum(gg_in[...], axis=0)
+
+    def flush_last(c):
+        @pl.when(c == 0)
+        def _():
+            flush(sz.full, sz.rem)
+
+    stored(0, 'own', tile_own, ship_own, flush_last)
+
+    with scope('t_gain'):
+        every(lambda k: heard_gain(k).wait_recv())
+    total = jnp.sum(gg_in[...], axis=0)
+    lse_sum = jnp.sum(st[2:3, :] * st[1:2, :], axis=1, keepdims=True)
+    gg_out[0:1, 0:gain.shape[1]] = total[0:1, 0:gain.shape[1]]
+    gg_out[0:1, gain.shape[1]:] = (lse_sum - total[0:1, gain.shape[1]:]) * (1.0 / LOG2E)
     every(lambda k: tell_gain(k).wait_send())
     put_own((sz.full - 1) % 2, 0, chunk).wait()
     put_own(sz.full % 2, 0, sz.rem).wait()
-    for slot, rows in (((sz.full - 1) % 2, chunk), (sz.full % 2, sz.rem)):
-        for cp in sends(slot, 0, rows):
+    with scope('t_send'):
+        def sent(c, _):
+            for cp in sends(c, chunk):
+                cp.wait_send()
+            return 0
+        lax.fori_loop(0, sz.full, sent, 0)
+        for cp in sends(sz.full, sz.rem):
             cp.wait_send()
     for q in (last - 2, last - 1):
         to_sib(q).wait_send()
@@ -700,6 +778,7 @@
         to_z(q).wait_send()
     to_x(rounds - 1).wait_send()
     for r in range(rounds):
+      with scope(f't_gather{r}'):
         keep(r).wait()
         for cp in gathers(r):
             cp.wait_send()
@@ -708,6 +787,7 @@
         for zf in range(n_z):
             rcopy(gh.at[r], home(zf * 2 + 1 - at.y, r), ag_s.at[r, 0], fw_r.at[r, zf], y_peer).wait_recv()
     for k in range(1, n):
+      with scope(f't_dw{k}'):
         src = lax.rem(me + n - k, n)
         rcopy(dw_hbm.at[pl.ds(0, sz.rows), :], dw_hbm.at[rows_at(src * sz.rows, sz.rows), :], dw_send.at[0, 0], dw_recv.at[k], sibling).wait_recv()
 
@@ -745,38 +825,37 @@
         lab_loc = jnp.where(mine, lab_all - tp_id * vocab_tp - fsdp_id * sz.rows, -1)[None, :]
         V = pltpu.VMEM
 
-        logits, z_all, w_blk, st = pl.pallas_call(
+        logits, z_all, w_blk, st, hit_sum = pl.pallas_call(
             functools.partial(logits_kernel, sz, n_tp, chunk, tok),
-            out_shape=(S((sz.rows, tokens), f32), S((tokens, d), bf16), S((sz.rows, d), bf16), S((8, tokens), f32)),
-            in_specs=[HBM, HBM, VM, VM, VM], out_specs=(HBM, HBM, HBM, VM),
+            out_shape=(S((sz.rows, tokens), f32), S((tokens, d), bf16), S((sz.rows, d), bf16), S((8, tokens), f32), S((1, 128), f32)),
+            in_specs=[HBM, HBM, VM, VM, VM], out_specs=(HBM, HBM, HBM, VM, VM),
             scratch_shapes=[V((tokens, d), bf16), V((sz.rows, d), bf16), V((chunk, tok), f32), V((chunk, tok), f32),
                             V((z_rows, d), bf16), V((z_rows, d), bf16),
                             V((8, tokens), f32), V((8, tokens), f32), V((8, tokens), f32),
-                            V((8, tokens), f32), V((n_all, 8, own), f32), V((8, own), f32), V((8, tokens), f32),
+                            V((2, tokens), f32), V((n_all, 2, own), f32), V((1, own), f32), V((1, tokens), f32),
                             DMA((sz.full + 2, n_fsdp)), DMA((sz.full + 2, n_fsdp)), DMA((sz.full + 2,)), DMA((2,)), DMA((2,)), DMA((2,)),
                             DMA((n_all,)), DMA((n_all,)), DMA((n_all,)), DMA((n_all,))],
             compiler_params=params(collective_id=0, has_side_effects=True), name='logits',
         )(hid_all, w_rows.T, norm_gain[None, :], lab_loc, scale)
 
-        mean_loss = jnp.sum(st[2])
         n_low = sz.full - early + 1
 
-        _, dw_t, grad_hidden, gain_sum = pl.pallas_call(
+        _, dw_t, grad_hidden, gain_sum, _ = pl.pallas_call(
             functools.partial(grad_kernel, sz, n_tp, chunk, early, tok, tok, half),
-            out_shape=(S((sz.rows, tokens), bf16), S((n_fsdp * sz.rows, width), bf16), S(hidden.shape, bf16), S((1, d), f32)),
-            in_specs=[HBM, HBM, HBM, VM, VM, VM, VM], out_specs=(HBM, HBM, HBM, VM),
+            out_shape=(S((sz.rows, tokens), bf16), S((n_fsdp * sz.rows, width), bf16), S(hidden.shape, bf16), S((1, d + 128), f32), S(((sz.full + 1) * chunk, 3 * width), bf16)),
+            in_specs=[HBM, HBM, HBM, VM, VM, VM, VM, VM], out_specs=(HBM, HBM, HBM, VM, HBM),
             scratch_shapes=[V((tokens, d), bf16), V((sz.rows, d), bf16), V((chunk, tok), f32), V((chunk, tok), f32), V((chunk, tok), bf16), V((chunk, tok), bf16),
                             V((sz.rows, 2 * half), bf16), V((sz.rows, 2 * half), bf16),
                             V((chunk, 3 * width), f32), V((2, chunk, 3 * width), bf16), V((chunk, width), f32), V((2, chunk, width), bf16),
                             V((2, 2 * half, d), bf16), V((2, 2 * half, d), bf16), V((2 * half, d), f32), V((2, half, d), bf16), V((8, half, d), bf16), V((3, half, d), f32),
-                            V((n_z - 1, half, d), bf16), V((rounds, 2, n_z - 1, half, d), bf16), V((2, half, d), f32), V((half, d), f32), V((rounds, half, d), f32),
-                            V((rounds, half, d), bf16), V((1, d), f32), V((n_all, 1, d), f32),
-                            DMA((1,)), DMA((1,)), DMA((2,)), DMA((2,)), DMA((2, 2)), DMA((2, 2 * n_low)), DMA((2, 2)),
-                            DMA((2, 3)), DMA((n_fsdp,)), DMA((2,)), DMA((2,)), DMA((2,)), DMA((2,)), DMA((8,)),
+                            V((n_z - 1, half, d), bf16), V((rounds, 2, n_z - 1, half, d), bf16), V((2, half, d), f32), V((half, d), bf16), V((rounds, half, d), bf16),
+                            V((rounds, half, d), bf16), V((1, d + 128), f32), V((n_all, 1, d + 128), f32),
+                            DMA((3,)), DMA((1,)), DMA((2,)), DMA((2,)), DMA((2, 2)), DMA((2, 2 * n_low)), DMA((2, 2)),
+                            DMA((2,)), DMA((sz.full + 1, 3)), DMA((n_fsdp,)), DMA((2,)), DMA((2,)), DMA((2,)), DMA((2,)), DMA((8,)),
                             DMA((n_z - 1,)), DMA((rounds, 2, n_z - 1)), DMA((1,)), DMA((rounds,)),
                             DMA((rounds, n_z)), DMA((rounds, n_z)), DMA((rounds, n_z)), DMA((rounds, n_z)), DMA((rounds,)), DMA((n_all,)), DMA((n_all,))],
             compiler_params=params(collective_id=1, has_side_effects=True), name='grads',
-        )(z_all, w_blk, logits, st, lab_loc, hid_own, norm_gain[None, :])
-        return mean_loss, grad_hidden, dw_t[:vocab_tp].T, gain_sum[0]
+        )(z_all, w_blk, logits, st, lab_loc, hid_own, norm_gain[None, :], hit_sum)
+        return gain_sum[0, d], grad_hidden, dw_t[:vocab_tp].T, gain_sum[0, :d]
 
     return jax.shard_map(per_device, mesh=mesh, in_specs=(P('fsdp', None), P('fsdp'), P('fsdp'), P(), P('fsdp', 'tp')), out_specs=(P(), P('fsdp', None), P('fsdp', 'tp'), P()), check_vma=False)

time: 597 us -> 562 us (0.941)
  the two profiles are of different devices: /device:TPU:0 before, /device:TPU:8 now
where the time goes in v3:
time: 562 us; the launch traced here: 561 us
  Pallas kernels  414 us (74%)
  waiting for transfers between devices  103 us (18%)
  local copies, waits for them, and re-layouts  17.1 us (3%)
  between operations  14.1 us (3%)
  blocking collectives  10.3 us (2%)
    pallas_call x1, Pallas kernels, per_device(): pl.pallas_call(functools.partial(grad_kernel, sz, n_tp, chunk, early, tok...  273 us
    pallas_call x1, Pallas kernels, per_device(): pl.pallas_call(functools.partial(logits_kernel, sz, n_tp, chunk, tok), ou...  141 us
    all_gather x1, waiting for transfers between devices, per_device(): hid_all = lax.all_gather(hid_own, everyone, axis=0, tiled=True)  103 us
  transfers between devices with their start and end apart: 1, of which 1 were waited for; matrix products, arithmetic and copies ran while one was open for 1% of the time, Pallas kernels for 0%

profile of v3, /device:TPU:8, one launch (start us, length us, event | category | flops | bytes accessed | tf_op | source)
XLA Modules:
  0.0 560.7 jit_solution(8940676151061700631)
XLA Ops:
  7.2 0.0 all-gather.2.cloned.1.call-start
  7.2 1.9 constant_dynamic-slice_fusion.hid
  9.1 0.0 all-gather.2.cloned.1.call-update
  9.1 1.3 broadcast_in_dim.12.gain
  10.4 5.2 all_gather.11
  15.6 0.6 reduce_sum.9
  16.2 5.2 all_gather.10
  21.3 1.3 broadcast_divide_fusion
  22.6 0.6 subtract_select_fusion
  23.2 102.9 %all-gather.2.cloned.1.call-done.h_hbm = bf16[8192,1024]{1,0:T(8,128)(2,1)} async-done(((bf16[256,1024]{1,0:T(8,128)(2,1)}), bf16[8192,1024]{1,0:T(8,128)(2,1)}) %all-gather.2.cloned.1.call-update) | async-done | bytes 16777232 | tf_op jit(solution)/shard_map/all_gather | solution.py:820
  126.1 141.0 %logits.1 = (f32[4752,8192]{1,0:T(8,128)}, bf16[8192,1024]{1,0:T(8,128)(2,1)}, bf16[4752,1024]{1,0:T(8,128)(2,1)}, f32[8,8192]{1,0:T(8,128)}, f32[1,128]{1,0:T(1,128)}) custom-call(bf16[8192,1024]{1,0:T(8,128)(2,1)} %all-gather.2.cloned.1.call-done.h_hbm, bf16[18992,256]{1,0:T(8,128)(2,1)} %bitcast.7, bf16[1,1024]{1,0:T(2,128)(2,1)} %broadcast_in_dim.12.gain, ...), custom_call_target="tpu_custom_call" | custom-call | tf_op jit(solution)/shard_map/logits/pallas_call | solution.py:828
  267.1 272.7 %grads.1 = (bf16[4752,8192]{1,0:T(8,128)(2,1)}, bf16[19008,256]{1,0:T(8,128)(2,1)}, bf16[2048,1024]{1,0:T(8,128)(2,1)}, f32[1,1152]{1,0:T(1,128)}, bf16[5120,768]{1,0:T(8,128)(2,1)}) custom-call(bf16[8192,1024]{1,0:T(8,128)(2,1)} %get-tuple-element.12.z_hbm, bf16[4752,1024]{1,0:T(8,128)(2,1)} %get-tuple-element.13.w_hbm, ...), custom_call_target="tpu_custom_call" | custom-call | tf_op jit(solution)/shard_map/grads/pallas_call | solution.py:843
  539.8 1.1 slice.9
  541.0 1.3 slice.11
  542.3 0.0 copy-start
  542.3 9.5 %slice_bitcast_fusion = bf16[256,18992]{0,1:T(8,128)(2,1)} fusion(bf16[19008,256]{1,0:T(8,128)(2,1)} %get-tuple-element.19), kind=kLoop, calls=%fused_computation | loop fusion | bytes 19447808 | tf_op jit(solution)/shard_map/transpose | solution.py:859
  551.8 0.0 copy-done
  551.8 2.0 copy.10
Async XLA Ops:
  7.2 118.9 %all-gather.2.cloned.1.call-start = ((), (), s32[]{:S(2)}) async-start(), calls=%async_computation | async-start | bytes 17301504 | tf_op jit(solution)/shard_map/all_gather | solution.py:820
  542.3 9.5 %copy-start = (bf16[2048,1024]{1,0:T(8,128)(2,1)S(1)}, bf16[2048,1024]{1,0:T(8,128)(2,1)}, u32[]{:S(2)}) copy-start(bf16[2048,1024]{1,0:T(8,128)(2,1)} %get-tuple-element.25) | copy-start | bytes 12582916
Sparse Core Ops, SparseCore 0:
  11.6 114.4 all-gather.1
